TPU v7x, 32 devices: a whole 2x2x4 slice. The times are simulated.
32 devices in a mesh: ctx: 8 (over z, core), fsdp: 4 (over y, x).
Axes of the slice: x: 2, y: 2, z: 4, core: 2. Of those that a mesh axis runs over, the one named last changes fastest.
Arguments:
- tokens: bfloat16 [4, 1024, 1024], P('fsdp', 'ctx'), may hold values from -6 to 6
- norm_first: bfloat16 [1024], P(('ctx', 'fsdp')), may hold values from 0.099609375 to 1.8984375
- w_query: bfloat16 [1024, 1024], P(('ctx', 'fsdp')), may hold values from -0.65625 to 0.65625
- w_key: bfloat16 [1024, 512], P(('ctx', 'fsdp')), may hold values from -0.65625 to 0.65625
- w_value: bfloat16 [1024, 512], P(('ctx', 'fsdp')), may hold values from -0.1875 to 0.1875
- w_out: bfloat16 [1024, 1024], P(('ctx', 'fsdp')), may hold values from -6 to 6
- norm_second: bfloat16 [1024], P(('ctx', 'fsdp')), may hold values from 0.099609375 to 1.8984375
- w_router: bfloat16 [1024, 32], P(('ctx', 'fsdp')), may hold values from -0.375 to 0.375
- w_gate: bfloat16 [32, 1024, 512], P('fsdp', 'ctx'), may hold values from -0.1875 to 0.1875
- w_up: bfloat16 [32, 1024, 512], P('fsdp', 'ctx'), may hold values from -0.1875 to 0.1875
- w_down: bfloat16 [32, 512, 1024], P('fsdp', None, 'ctx'), may hold values from -2.390625 to 2.390625
- positions: int32 [4, 1024], P('fsdp', 'ctx'), may hold values from 0 to 1023, as said below
- routes: int32 [4, 1024, 8], P('fsdp', 'ctx'), may hold values from 0 to 31, all different within a row; in each aligned block of 128 rows (0 to 127, 128 to 255, ..., all dimensions but the last counted through in order) at most 48 rows name the same one
- cotangent: bfloat16 [4, 1024, 1024], P('fsdp', 'ctx'), may hold values from -6 to 6
Outputs:
- output: bfloat16 [4, 1024, 1024], P('fsdp', 'ctx')
- grad_tokens: float32 [4, 1024, 1024], P('fsdp', 'ctx')
- grad_norm_first: float32 [1024], P(('ctx', 'fsdp'))
- grad_query: float32 [1024, 1024], P(('ctx', 'fsdp'))
- grad_key: float32 [1024, 512], P(('ctx', 'fsdp'))
- grad_value: float32 [1024, 512], P(('ctx', 'fsdp'))
- grad_out: float32 [1024, 1024], P(('ctx', 'fsdp'))
- grad_norm_second: float32 [1024], P(('ctx', 'fsdp'))
- grad_router: float32 [1024, 32], P(('ctx', 'fsdp'))
- grad_gate: float32 [32, 1024, 512], P('fsdp', 'ctx')
- grad_up: float32 [32, 1024, 512], P('fsdp', 'ctx')
- grad_down: float32 [32, 512, 1024], P('fsdp', None, 'ctx')
Inputs may be any that keep to these rules, and one draw needn't show every extreme that they name: Each sequence's positions are a permutation of 0 to 1023, made of runs of 64 consecutive increasing positions in an order drawn per sequence. `routes`: each row names 8 different experts; within the rows of one device (aligned blocks of 128 rows, sequences in order) no expert is named by more than 48 rows.
All inputs are finite; a program needn't handle non-finite values.
Results may differ from a plain program's by a relative error of at most 0.025.
The roundings to bfloat16 on the way count: a program that leaves them out, or rounds other values in their place, can miss the bound.
Values may be sent and summed in bfloat16 or wider, within the bound.
A program may use at most 192 MiB of HBM per device.

v0:
```python
import collections
import functools
import types

import jax
import jax.numpy as jnp
import numpy as np
from jax import lax
from jax.experimental import pallas as pl
from jax.experimental.pallas import tpu as pltpu
from jax.sharding import PartitionSpec as P

D = 1024
HEADS = 16
KV_HEADS = 8
HEAD = 64
EXPERTS = 32
TOP = 8
CAP = 48
LANES = 128

residual_scale = 0.22
score_scale = 0.015625
rope_base = 10000.0
norm_eps = 1e-06
masked_score = -1e30

MESH = pl.DeviceIdType.MESH
Place = collections.namedtuple("Place", ["c", "f", "m", "s", "h", "k", "p", "w"])


class Sizes:
    def __init__(self, mesh):
        self.C = mesh.shape["ctx"]
        self.F = mesh.shape["fsdp"]
        self.N = self.C * self.F
        self.G = EXPERTS // self.F
        self.S = self.C // self.G
        self.H = self.G // 2
        self.P = 2 * self.F
        self.J = self.C // 2
        self.q_heads = HEADS // self.C
        self.q_width = self.q_heads * HEAD
        self.share = self.C // KV_HEADS
        self.rows_w = D // self.N

    def place(self, c, f):
        k = lax.rem(c, 2)
        return Place(c, f, lax.rem(c, self.G), lax.div(c, self.G), lax.rem(lax.div(c, 2), self.H), k, f * 2 + k, c * self.F + f)

    def count(self, group):
        return {"ctx": self.C, "fsdp": self.F, "world": self.N, "col": self.H, "line": self.J, "plane": self.P}[group]

    def peer(self, group, me, n):
        if group == "ctx":
            return self.place(lax.rem(me.c + n, self.C), me.f)
        if group == "fsdp":
            return self.place(me.c, lax.rem(me.f + n, self.F))
        if group == "world":
            w = lax.rem(me.w + n, self.N)
            return self.place(lax.div(w, self.F), lax.rem(w, self.F))
        if group == "col":
            return self.place(me.s * self.G + 2 * lax.rem(me.h + n, self.H) + me.k, me.f)
        if group == "line":
            return self.place(2 * lax.rem(lax.div(me.c, 2) + n, self.J) + me.k, me.f)
        p = lax.rem(me.p + n, self.P)
        return self.place(me.s * self.G + 2 * me.h + lax.rem(p, 2), lax.div(p, 2))

    def expert(self, me, p):
        return lax.div(p, 2) * self.G + 2 * me.h + lax.rem(p, 2)


def bf(x):
    return x.astype(jnp.bfloat16)


def f32(x):
    return x.astype(jnp.float32)


def shape_of(shape, dtype=jnp.bfloat16):
    return jax.ShapeDtypeStruct(shape, dtype)


class Lane:
    def __init__(self, sizes, me, group, src, dst, sends, recvs):
        self.sizes, self.me, self.group, self.src, self.dst = sizes, me, group, src, dst
        self.sends, self.recvs, self.n = sends, recvs, sizes.count(group)

    def copy(self, k, to, source, landing):
        return pltpu.make_async_remote_copy(
            src_ref=source, dst_ref=landing, send_sem=self.sends.at[k], recv_sem=self.recvs.at[k],
            device_id=(to.c, to.f), device_id_type=MESH)

    def to(self, k):
        return self.sizes.peer(self.group, self.me, k)

    def start_one(self, k):
        to = self.to(k)
        self.copy(k, to, self.src(to), self.dst(self.me)).start()

    def wait_recv_one(self, k):
        landed = self.dst(self.sizes.peer(self.group, self.me, self.n - k))
        self.copy(k, self.to(k), landed, landed).wait_recv()

    def wait_send_one(self, k):
        to = self.to(k)
        self.copy(k, to, self.src(to), self.dst(self.me)).wait_send()

    def each(self, step):
        def one(k, carry):
            step(k)
            return carry
        lax.fori_loop(1, self.n, one, 0)

    def start(self):
        self.each(self.start_one)

    def wait_recv(self):
        self.each(self.wait_recv_one)

    def wait_send(self):
        self.each(self.wait_send_one)


class Relay:
    def __init__(self, sizes, me, own, landing, sends, recvs):
        self.sizes, self.me, self.own, self.landing, self.sends, self.recvs = sizes, me, own, landing, sends, recvs

    def member(self, n, core):
        J = self.sizes.J
        return 2 * lax.rem(lax.div(self.me.c, 2) + J - n, J) + core

    def copy(self, n, source, landing):
        return pltpu.make_async_remote_copy(
            src_ref=source, dst_ref=landing, send_sem=self.sends.at[n], recv_sem=self.recvs.at[n],
            device_id=(self.me.c + 1 - 2 * self.me.k, self.me.f), device_id_type=MESH)

    def start_own(self):
        self.copy(0, self.own, self.landing(self.me.c)).start()

    def start_one(self, n):
        here = self.landing(self.member(n, self.me.k))
        self.copy(n, here, here).start()

    def wait_recv_one(self, n):
        there = self.landing(self.member(n, 1 - self.me.k))
        self.copy(n, there, there).wait_recv()

    def wait_send(self):
        def one(n, carry):
            here = self.landing(self.member(n, self.me.k))
            self.copy(n, here, here).wait_send()
            return carry
        lax.fori_loop(0, self.sizes.J, one, 0)


def meet(sizes, me, groups):
    barrier = pltpu.get_barrier_semaphore()
    total = 0
    for group in groups:
        def greet(k, carry, group=group):
            p = sizes.peer(group, me, k)
            pl.semaphore_signal(barrier, inc=1, device_id=(p.c, p.f), device_id_type=MESH)
            return carry
        lax.fori_loop(1, sizes.count(group), greet, 0)
        total += sizes.count(group) - 1
    pl.semaphore_wait(barrier, total)


def times(n, step, first=0):
    def one(i, carry):
        step(i)
        return carry
    lax.fori_loop(first, n, one, 0)


def column_lane(z, me, c, source, landing, sends, recvs):
    return Lane(z, me, "fsdp", lambda to: source(c, to), lambda p: landing(c, p), sends.at[c], recvs.at[c])


def nn(a, b):
    return lax.dot_general(a, b, (((1,), (0,)), ((), ())), preferred_element_type=jnp.float32)


def nt(a, b):
    return lax.dot_general(a, b, (((1,), (1,)), ((), ())), preferred_element_type=jnp.float32)


def tn(a, b):
    return lax.dot_general(a, b, (((0,), (0,)), ((), ())), preferred_element_type=jnp.float32)


def lane_of(shape):
    return lax.broadcasted_iota(jnp.int32, shape, 1)


def rope_tables(place_columns, frequency):
    angles = place_columns.astype(jnp.float32) * frequency
    return jnp.cos(angles), jnp.sin(angles)


def rope(x, cosine, sine):
    half = HEAD // 2
    mixed = jnp.where(lax.rem(lane_of(x.shape), HEAD) < half, -pltpu.roll(x, LANES - half, 1), pltpu.roll(x, half, 1))
    return x * cosine + mixed * sine


def rows_at(ref, i, n):
    return ref.at[pl.ds(pl.multiple_of(i * n, n), n), :]


def vmem(shape, dtype=jnp.bfloat16):
    return pltpu.VMEM(shape, dtype)


def frequencies():
    lanes = np.arange(LANES)
    steps = rope_base ** ((lanes % (HEAD // 2)) * (-2.0 / HEAD))
    return jnp.asarray(np.stack([steps, np.where(lanes < HEAD, steps, 0.0)] + [steps] * 6), jnp.float32)


def exact(kind, a, b):
    dims = {"nn": ((1,), (0,)), "nt": ((1,), (1,)), "tn": ((0,), (0,))}[kind]
    return lax.dot_general(a, b, (dims, ((), ())), precision=lax.Precision.HIGHEST, preferred_element_type=jnp.float32)


LANE_GROUPS = dict(
    tok="line", place="ctx", wc="ctx", small="ctx", wo="line", cot="col", slot="col", gate_a="ctx", gate_b="ctx", up="ctx",
    down="ctx", att="ctx", rows="col", gates="col", part="col", turn="col", d_attn="line", mix="col", dn="line", gc="ctx",
    gs="ctx", go="fsdp", grad0="ctx", grad1="ctx", grad2="ctx", grad3="ctx", grad4="ctx", grad5="ctx")
PLANE_LANES = ["cot", "row", "g", "back", "dg", "out"]
COLUMN_LANES = ["wc", "small", "wo", "gc", "gs"]
RELAYS = ["tok", "wo", "d_attn", "sib"]


def layer_kernel(z, R, dc, tile, names, *refs):
    r = types.SimpleNamespace(**dict(zip(names, refs)))
    me = z.place(lax.axis_index("ctx"), lax.axis_index("fsdp"))
    C, F, H, P, J, rs, qw = z.C, z.F, z.H, z.P, z.J, z.rows_w, z.q_width
    L = C * R
    half = dc // 2
    low, high = pl.ds(0, half), pl.ds(half, half)
    sems = lambda kind, name: (getattr(r, kind + name + "_send"), getattr(r, kind + name + "_recv"))

    def at_slot(ref, h, p):
        return rows_at(ref, h * P + p, CAP)

    def lane(name, source, landing):
        return Lane(z, me, LANE_GROUPS[name], source, landing, *sems("lane_", name))

    def plane(name, source, landing):
        def at(h):
            send, recv = sems("plane_", name)
            land = lambda p: at_slot(landing, h, p.p) if len(landing.shape) == 2 else landing.at[h, p.p]
            return Lane(z, me, "plane", lambda to: source.at[h, to.p], land, send.at[h], recv.at[h])
        return at

    def column(name, source, landing):
        return lambda c: column_lane(z, me, c, source, landing, *sems("column_", name))

    def relay(name, own, landing):
        return Relay(z, me, own, landing, *sems("relay_", name))

    tok_lane = lane("tok", lambda to: r.tok, lambda p: r.blocks.at[p.c])
    tok_relay = relay("tok", r.tok, lambda c: r.blocks.at[c])
    place_lane = lane("place", lambda to: r.place, lambda p: r.place_all.at[p.c])
    wc_lane = lane("wc", lambda to: r.w_pack.at[to.c], lambda p: rows_at(r.wc_v, p.w, rs))
    small_lane = lane("small", lambda to: r.small, lambda p: rows_at(r.small_v, p.w, rs))
    wo_lane = lane("wo", lambda to: r.w_out, lambda p: rows_at(r.wo_v, p.w, rs))
    wo_relay = relay("wo", r.w_out, lambda c: rows_at(r.wo_v, c * F + me.f, rs))
    spread = lambda name, ref: column(
        name, lambda c, to: rows_at(ref, c * F + me.f, rs), lambda c, p: rows_at(ref, c * F + p.f, rs))
    wc_column, small_column, wo_column = spread("wc", r.wc_v), spread("small", r.small_v), spread("wo", r.wo_v)
    cot_lane = lane("cot", lambda to: r.cot, lambda p: r.cot_all.at[p.h])
    slot_lane = lane("slot", lambda to: r.slot_t.at[pl.ds(0, EXPERTS), :], lambda p: r.slot_all.at[p.h])
    gate_a_lane = lane("gate_a", lambda to: r.w_gate.at[to.m, low], lambda p: r.wv.at[0, p.c, low])
    gate_b_lane = lane("gate_b", lambda to: r.w_gate.at[to.m, high], lambda p: r.wv.at[0, p.c, high])
    up_lane = lane("up", lambda to: r.w_up.at[to.m], lambda p: r.wv.at[1, p.c])
    down_lane = lane("down", lambda to: r.w_downt.at[to.m], lambda p: r.wv.at[2, p.c])
    att_lane = lane("att", lambda to: r.att_stage.at[to.c], lambda p: r.att_in.at[p.c])
    rows_lane = lane("rows", lambda to: r.h2, lambda p: r.h_all.at[p.h])
    gates_lane = lane("gates", lambda to: r.gates_t.at[pl.ds(0, EXPERTS), :], lambda p: r.gate_all.at[p.h])
    part_lane = lane("part", lambda to: r.part_stage.at[to.h], lambda p: r.part_in.at[p.h])
    turn_lane = lane("turn", lambda to: r.turn_stage.at[to.h], lambda p: r.turn_in.at[p.h])
    up_attn_lane = lane("d_attn", lambda to: r.d_attn, lambda p: r.blocks.at[p.c])
    up_attn_relay = relay("d_attn", r.d_attn, lambda c: r.blocks.at[c])
    mix_lane = lane("mix", lambda to: r.part_stage.at[to.h], lambda p: r.mix_in.at[p.h])
    dn_block = lambda c: rows_at(r.pool, c, R)
    dn_in = lambda j: rows_at(r.xin, j, R)
    sib_in = lambda j: rows_at(r.cot_v, j, R)
    dn_lane = lane("dn", lambda to: dn_block(to.c), lambda p: dn_in(lax.div(p.c, 2)))
    gc_lane = lane("gc", lambda to: r.gc_sum.at[to.c], lambda p: r.gc_in.at[p.c])
    gs_lane = lane("gs", lambda to: r.gs_sum.at[to.c], lambda p: r.gs_in.at[p.c])
    go_lane = lane("go", lambda to: rows_at(r.go_stage, to.f, rs), lambda p: r.go_in.at[p.f])
    gather = lambda name, stage, landing: column(
        name, lambda c, to: rows_at(stage, c * F + to.f, rs), lambda c, p: landing.at[p.f, c])
    gc_column, gs_column = gather("gc", r.gc_stage, r.gc_x), gather("gs", r.gs_stage, r.gs_x)
    grad_lanes = [
        lane("grad" + str(2 * j + i),
             lambda to, j=j, i=i: r.wv.at[j, to.c, (low, high)[i]],
             lambda p, j=j, i=i: r.gw_in.at[j, p.s, p.m, (low, high)[i]])
        for j in range(3) for i in range(2)
    ]
    cot_plane = plane("cot", r.d_rows, r.cot_v)
    row_plane = plane("row", r.stage, r.xin)
    g_plane = plane("g", r.g_stage, r.gin)
    back_plane = plane("back", r.d_rows, r.stage)
    dg_plane = plane("dg", r.dg_stage, r.dg_in)
    out_plane = plane("out", r.result, r.out_in)

    def sib_copy(j):
        send, recv = sems("relay_", "sib")
        return pltpu.make_async_remote_copy(
            src_ref=dn_block(2 * j + 1 - me.k), dst_ref=sib_in(j), send_sem=send.at[j], recv_sem=recv.at[j],
            device_id=(me.c + 1 - 2 * me.k, me.f), device_id_type=MESH)

    meet(z, me, ["ctx", "plane", "fsdp"])
    wc_lane.start()
    small_lane.start()
    place_lane.start()
    tok_relay.start_own()
    tok_lane.start()

    own = [
        pltpu.make_async_copy(r.w_pack.at[me.c], rows_at(r.wc_v, me.w, rs), r.own_sem.at[0]),
        pltpu.make_async_copy(r.small, rows_at(r.small_v, me.w, rs), r.own_sem.at[1]),
        pltpu.make_async_copy(r.w_out, rows_at(r.wo_v, me.w, rs), r.own_sem.at[2]),
    ]
    own_weights = [
        pltpu.make_async_copy(source.at[me.m], r.wv.at[j, me.c], r.own_sem.at[3 + j])
        for j, source in enumerate([r.w_gate, r.w_up, r.w_downt])
    ]
    for copy in own + own_weights:
        copy.start()
    r.blocks[me.c] = r.tok[...]
    r.place_all[me.c] = r.place[...]
    r.cot_all[me.h] = r.cot[...]

    named = jnp.zeros((R, LANES), jnp.float32)
    for j in range(TOP):
        named = jnp.where(r.routes[:, j : j + 1] == lane_of((R, LANES)), 1.0, named)
    row_id = lax.broadcasted_iota(jnp.int32, (R, R), 0)
    before = jnp.where(row_id > lane_of((R, R)), 1.0, 0.0).astype(jnp.bfloat16)
    slot = nn(before, named.astype(jnp.bfloat16))
    r.slot_t[...] = jnp.where(named > 0.5, slot, -1.0).T
    r.slot_all[me.h] = r.slot_t[0:EXPERTS, :]
    slot_lane.start()
    slot_id = lax.broadcasted_iota(jnp.int32, (CAP, R), 0).astype(jnp.float32)

    for copy in own:
        copy.wait()
    wc_lane.wait_recv()
    times(C, lambda c: wc_column(c).start())
    small_lane.wait_recv()
    times(C, lambda c: small_column(c).start())

    def dispatch_cot(j):
        h = lax.rem(me.h + H - j, H)
        @pl.when(j > 0)
        def _():
            cot_lane.wait_recv_one(j)
            slot_lane.wait_recv_one(j)

        def to_expert(n):
            p = lax.rem(me.p + n, P)
            row = r.slot_all[h, pl.ds(z.expert(me, p), 1), :]
            hot = jnp.where(row == slot_id, 1.0, 0.0).astype(jnp.bfloat16)
            r.pick[h, p] = hot
            r.d_rows[h, p] = nn(hot, r.cot_all[h]).astype(jnp.bfloat16)
            @pl.when(n > 0)
            def _():
                cot_plane(h).start_one(n)
        times(P, to_expert)
        at_slot(r.cot_v, h, me.p)[...] = r.d_rows[h, me.p]
    dispatch_cot(0)
    place_lane.wait_recv()
    times(C, lambda c: wc_column(c).wait_recv())
    times(C, lambda c: small_column(c).wait_recv())
    gain_one = r.small_v[...].astype(jnp.float32).T[EXPERTS : EXPERTS + 1, :]
    gain_two = r.small_v[...].astype(jnp.float32).T[EXPERTS + 1 : EXPERTS + 2, :]
    head_of = lax.div(lane_of((R, LANES)), HEAD)

    def project(i):
        n = lax.rem(i, J)
        c = tok_relay.member(n, jnp.where(i < J, me.k, 1 - me.k))
        @pl.when(jnp.logical_and(i > 0, i < J))
        def _():
            tok_lane.wait_recv_one(n)
            tok_relay.start_one(n)
        @pl.when(i >= J)
        def _():
            tok_relay.wait_recv_one(n)
        x = r.blocks[c].astype(jnp.float32)
        inverse = lax.rsqrt(jnp.mean(x * x, axis=-1, keepdims=True) + norm_eps)
        h = (x * inverse * gain_one).astype(jnp.bfloat16)
        part = pl.ds(pl.multiple_of(c * R, R), R)
        r.h1[part, :] = h
        qkv = nn(h, r.wc_v[...])
        row = r.place_all[c][0:1, :].astype(jnp.float32)
        r.place_row[c] = jnp.broadcast_to(row, (8, R))
        places = jnp.broadcast_to(row, (R, R)).T
        r.place_col[part, :] = places
        r.q_all[part, :] = rope(qkv[:, :LANES], *rope_tables(places, r.freq[0:1, :])).astype(jnp.bfloat16)
        kv = rope(qkv[:, LANES:], *rope_tables(places, r.freq[1:2, :]))
        swapped = pltpu.roll(kv, HEAD, 1)
        r.k2[part, :] = jnp.where(head_of == 0, kv, swapped).astype(jnp.bfloat16)
        r.v2[part, :] = jnp.where(head_of == 0, swapped, kv).astype(jnp.bfloat16)
    times(C, project)
    wo_relay.start_own()
    wo_lane.start()
    cot_lane.start()
    tok_relay.wait_send()

    def attend(c):
        part = pl.ds(pl.multiple_of(c * R, R), R)
        q = r.q_all[part, :]
        row = jnp.concatenate([r.place_row[i, 0:1, :] for i in range(C)], axis=1)
        allowed = row <= r.place_col[part, 0:1]
        total = jnp.zeros((R, LANES), jnp.float32)
        for h in range(z.q_heads):
            mine = head_of == h
            s = nt(jnp.where(mine, q, jnp.zeros_like(q)), r.k2[...]) * score_scale
            s = jnp.where(allowed, s, masked_score)
            top = jnp.max(s, axis=-1, keepdims=True)
            e = jnp.exp(s - top)
            weight = jnp.sum(e, axis=-1, keepdims=True)
            r.lse[h, part, :] = jnp.broadcast_to(top + jnp.log(weight), (R, LANES))
            total = jnp.where(mine, nn(e.astype(jnp.bfloat16), r.v2[...]) / weight, total)
        r.att_f[part, :] = total
        r.att_stage[c] = total.astype(jnp.bfloat16)
    times(C // 2, attend)
    wo_lane.wait_recv()
    times(J, wo_relay.start_one, 1)
    times(C, attend, C // 2)
    att_lane.start()
    gate_a_lane.start()
    r.att_in[me.c] = r.att_stage[me.c]
    times(J, wo_relay.wait_recv_one)
    times(C, lambda c: wo_column(c).start())
    times(H, dispatch_cot, 1)
    att_lane.wait_recv()
    times(C, lambda c: wo_column(c).wait_recv())
    x = r.tok[...].astype(jnp.float32)
    mixed = jnp.zeros((R, D), jnp.float32)
    for c in range(C):
        mixed = mixed + nn(r.att_in[c][:, :qw], r.wo_v[c * qw : (c + 1) * qw, :])
    mid = x + residual_scale * mixed
    r.middle[...] = mid
    inverse = lax.rsqrt(jnp.mean(mid * mid, axis=-1, keepdims=True) + norm_eps)
    hidden = (mid * inverse * gain_two).astype(jnp.bfloat16)
    r.h2[...] = hidden
    rows_lane.start()
    chosen = r.slot_t[...].T > -0.5
    logits = jnp.where(chosen, nn(hidden, r.small_v[...]), masked_score)
    raised = jnp.where(chosen, jnp.exp(logits - jnp.max(logits, axis=-1, keepdims=True)), 0.0)
    r.gates_t[...] = (raised / jnp.sum(raised, axis=-1, keepdims=True)).T
    gates_lane.start()
    gate_b_lane.start()
    up_lane.start()
    down_lane.start()
    r.h_all[me.h] = r.h2[...]
    r.gate_all[me.h] = r.gates_t[0:EXPERTS, :]

    def dispatch_rows(j):
        h = lax.rem(me.h + H - j, H)
        @pl.when(j > 0)
        def _():
            rows_lane.wait_recv_one(j)
            gates_lane.wait_recv_one(j)

        def to_expert(n):
            p = lax.rem(me.p + n, P)
            hot = r.pick[h, p]
            r.stage[h, p] = nn(hot, r.h_all[h]).astype(jnp.bfloat16)
            g = jnp.broadcast_to(r.gate_all[h, pl.ds(z.expert(me, p), 1), :], (8, R))
            wide = jnp.concatenate([hot.astype(jnp.float32), jnp.zeros((LANES - CAP, R), jnp.float32)], axis=0)
            r.g_stage[h, p] = exact("nt", g, wide)
            @pl.when(n > 0)
            def _():
                row_plane(h).start_one(n)
        times(P, to_expert)
        at_slot(r.xin, h, me.p)[...] = r.stage[h, me.p]
        r.gin[h, me.p] = r.g_stage[h, me.p]
    times(H, dispatch_rows)

    def send_gates(j):
        h = lax.rem(me.h + H - j, H)

        def to_expert(n):
            row_plane(h).wait_send_one(n)
            g_plane(h).start_one(n)
        times(P, to_expert, 1)
    times(H, send_gates)
    times(H, lambda h: cot_plane(h).wait_send())
    for copy in own_weights:
        copy.wait()
    for bulk in [gate_a_lane, gate_b_lane, up_lane, down_lane]:
        bulk.wait_recv()
    times(H, lambda h: cot_plane(h).wait_recv())
    wg, wu, wd = [r.wv.at[j].reshape(D, r.wv.shape[3]) for j in range(3)]
    per = tile // CAP

    def chunk(j):
        h = lax.rem(me.h + H - lax.rem(j + 1, H), H)
        row_plane(h).wait_recv()
        g_plane(h).wait_recv()

        def rows(t):
            some = pl.ds(pl.multiple_of(t * per, per), per)
            part = pl.ds(pl.multiple_of((h * P + t * per) * CAP, CAP), tile)
            for p in range(per):
                turned = jnp.broadcast_to(r.gin[h, t * per + p, 0:1, :], (LANES, LANES)).T
                r.g_col[p * CAP : (p + 1) * CAP, :] = turned[0:CAP, :]
            x = r.xin[part, :]
            gate = nn(x, wg[...])
            up = nn(x, wu[...])
            sig = jax.nn.sigmoid(gate)
            act = gate * sig
            hidden = (act * up).astype(jnp.bfloat16)
            r.hid[part, :] = hidden
            out = nt(hidden, wd[...]).astype(jnp.bfloat16)
            r.result[h, some] = out.reshape(per, CAP, D)
            upstream = r.cot_v[part, :].astype(jnp.float32)
            d_gates = residual_scale * jnp.sum(upstream * out.astype(jnp.float32), axis=-1, keepdims=True)
            d_out = (residual_scale * r.g_col[:, 0:1] * upstream).astype(jnp.bfloat16)
            r.pool[part, :] = d_out
            d_hidden = nn(d_out, wd[...])
            dg = (d_hidden * up * sig * (1.0 + gate * (1.0 - sig))).astype(jnp.bfloat16)
            du = (d_hidden * act).astype(jnp.bfloat16)
            r.d_gate[part, :] = dg
            r.d_up[part, :] = du
            r.d_rows[h, some] = (nt(dg, wg[...]) + nt(du, wu[...])).astype(jnp.bfloat16).reshape(per, CAP, D)
            r.g_col[...] = jnp.broadcast_to(d_gates, (tile, LANES))
            for p in range(per):
                turned = jnp.concatenate(
                    [r.g_col[p * CAP : (p + 1) * CAP, :], jnp.zeros((LANES - CAP, LANES), jnp.float32)], axis=0)
                r.dg_stage[h, t * per + p] = turned.T[0:8, :]
        times(P // per, rows)
        back_plane(h).start()
        dg_plane(h).start()
        r.stage[h, me.p] = r.d_rows[h, me.p]
        r.dg_in[h, me.p] = r.dg_stage[h, me.p]
    times(H, chunk)
    times(H, lambda h: out_plane(h).start())
    own_out = pltpu.make_async_copy(r.result.at[:, me.p], r.out_in.at[:, me.p], r.own_sem.at[7])
    own_out.start()

    def cut(d):
        part = pl.ds(pl.multiple_of(d * 256, 256), 256)
        x = r.xin[:, part]
        wg[part, :] = tn(x, r.d_gate[...]).astype(jnp.bfloat16)
        wu[part, :] = tn(x, r.d_up[...]).astype(jnp.bfloat16)
        wd[part, :] = tn(r.pool[pl.ds(0, H * P * CAP), part], r.hid[...]).astype(jnp.bfloat16)
    times(D // 256, cut)
    grad_lanes[0].start()
    own_grads = [
        pltpu.make_async_copy(r.wv.at[j, me.c], r.gw_in.at[j, me.s, me.m], r.own_sem.at[8 + j]) for j in range(3)
    ]
    for copy in own_grads:
        copy.start()

    def collect(j):
        n = lax.rem(j + 1, H)
        h = lax.rem(me.h + H - n, H)
        back_plane(h).wait_recv()
        dg_plane(h).wait_recv()
        part = tn(r.pick[h].reshape(P * CAP, R), r.stage[h].reshape(P * CAP, D))
        r.turn_stage[h] = jnp.zeros((EXPERTS, R), jnp.float32)

        def gates_of(p):
            row = jnp.broadcast_to(r.dg_in[h, p, 0:1, 0:CAP], (8, CAP))
            r.turn_stage[h, pl.ds(z.expert(me, p), 1), :] = exact("nn", row, r.pick[h, p].astype(jnp.float32))[0:1, :]
        times(P, gates_of)
        @pl.when(n > 0)
        def _():
            r.part_stage[h] = part.astype(jnp.bfloat16)
            part_lane.start_one(H - n)
            turn_lane.start_one(H - n)
        @pl.when(n == 0)
        def _():
            r.d_mid[...] = part
            r.turn_v[...] = jnp.zeros((LANES, R), jnp.float32)
            r.turn_v[0:EXPERTS, :] = r.turn_stage[h]
    times(H, collect)
    grad_lanes[1].start()
    part_lane.wait_recv()
    turn_lane.wait_recv()

    def add_part(n):
        h = lax.rem(me.h + n + 1, H)
        r.d_mid[...] += r.part_in[h].astype(jnp.float32)
        r.turn_v[0:EXPERTS, :] += r.turn_in[h]
    times(H - 1, add_part)
    gts = r.gates_t[...].T
    dgs = r.turn_v[...].T
    d_log = gts * (dgs - jnp.sum(gts * dgs, axis=-1, keepdims=True))
    d_h2 = r.d_mid[...] + exact("nt", d_log, r.small_v[...].astype(jnp.float32))
    mid = r.middle[...]
    inverse = lax.rsqrt(jnp.mean(mid * mid, axis=-1, keepdims=True) + norm_eps)
    n2 = mid * inverse
    g = d_h2 * gain_two
    dm = r.cot[...].astype(jnp.float32) + inverse * (g - n2 * jnp.mean(g * n2, axis=-1, keepdims=True))
    r.d_mid[...] = dm
    r.d_attn[...] = (residual_scale * dm).astype(jnp.bfloat16)
    up_attn_relay.start_own()
    up_attn_lane.start()
    grad_lanes[2].start()
    r.gain_v[...] = jnp.zeros((LANES, D), jnp.float32)
    r.gain_v[EXPERTS + 1 : EXPERTS + 2, :] = jnp.sum(d_h2 * n2, axis=0, keepdims=True)
    r.g_small[...] = exact("tn", r.h2[...].astype(jnp.float32), d_log)

    r.blocks[me.c] = r.d_attn[...]
    r.dk_acc[...] = jnp.zeros((L, LANES), jnp.float32)
    r.dv_acc[...] = jnp.zeros((L, LANES), jnp.float32)
    wo_c = rows_at(r.wo_v, me.c, qw)

    def attend_back(i):
        n = lax.rem(i, J)
        c = up_attn_relay.member(n, jnp.where(i < J, me.k, 1 - me.k))
        @pl.when(jnp.logical_and(i > 0, i < J))
        def _():
            up_attn_lane.wait_recv_one(n)
            up_attn_relay.start_one(n)
        @pl.when(i >= J)
        def _():
            up_attn_relay.wait_recv_one(n)
        part = pl.ds(pl.multiple_of(c * R, R), R)
        q = r.q_all[part, :]
        d_mix = nt(r.blocks[c], wo_c[...])
        if qw < LANES:
            d_mix = jnp.concatenate([d_mix, jnp.zeros((R, LANES - qw), jnp.float32)], axis=1)
        d_mix = d_mix.astype(jnp.bfloat16)
        row = jnp.concatenate([r.place_row[i, 0:1, :] for i in range(C)], axis=1)
        places = r.place_col[part, :]
        allowed = row <= places[:, 0:1]
        dq = jnp.zeros((R, LANES), jnp.float32)
        for h in range(z.q_heads):
            mine = head_of == h
            rows = pl.ds(h * R, R)
            q_h = jnp.where(mine, q, jnp.zeros_like(q))
            dm_h = jnp.where(mine, d_mix, jnp.zeros_like(d_mix))
            r.q_v[rows, :] = q_h
            r.dm_v[rows, :] = dm_h
            s = jnp.where(allowed, nt(q_h, r.k2[...]) * score_scale, masked_score)
            p = jnp.exp(s - r.lse[h, part, 0:1])
            r.p_v[rows, :] = p.astype(jnp.bfloat16)
            delta = jnp.sum(dm_h.astype(jnp.float32) * r.att_f[part, :], axis=-1, keepdims=True)
            ds = (p * (nt(dm_h, r.v2[...]) - delta)).astype(jnp.bfloat16)
            r.ds_v[rows, :] = ds
            dq = jnp.where(mine, nn(ds, r.k2[...]) * score_scale, dq)
        r.dk_acc[...] += tn(r.ds_v[...], r.q_v[...])
        r.dv_acc[...] += tn(r.p_v[...], r.dm_v[...])
        cosine, sine = rope_tables(places, r.freq[0:1, :])
        r.d_qkv[part, 0:LANES] = rope(dq, cosine, -sine).astype(jnp.bfloat16)
    times(C, attend_back)

    def finish_kv(c):
        part = pl.ds(pl.multiple_of(c * R, R), R)
        dk = r.dk_acc[part, :] * score_scale
        dv = r.dv_acc[part, :]
        dk = dk + pltpu.roll(dk, HEAD, 1)
        dv = dv + pltpu.roll(dv, HEAD, 1)
        cosine, sine = rope_tables(r.place_col[part, :], r.freq[1:2, :])
        r.d_qkv[part, LANES : 2 * LANES] = rope(jnp.where(head_of == 0, dk, dv), cosine, -sine).astype(jnp.bfloat16)
    times(C, finish_kv)

    def down_tokens(c):
        return nt(r.d_qkv[pl.ds(pl.multiple_of(c * R, R), R), :], r.wc_v[...])

    def for_sibling(j):
        c = 2 * j + 1 - me.k
        dn_block(c)[...] = down_tokens(c).astype(jnp.bfloat16)
        sib_copy(j).start()
    times(J, for_sibling)

    def for_line(i):
        n = lax.rem(i + 1, J)
        to = z.peer("line", me, n)
        dn = down_tokens(to.c)
        j = lax.div(to.c, 2)
        sib_copy(j).wait_recv()
        dn_block(to.c)[...] = (dn + sib_in(j)[...].astype(jnp.float32)).astype(jnp.bfloat16)
        @pl.when(n > 0)
        def _():
            dn_lane.start_one(n)
    times(J, for_line)
    dn_in(lax.div(me.c, 2))[...] = dn_block(me.c)[...]

    own_out.wait()
    part_lane.wait_send()

    def mix(i):
        n = lax.rem(i + 1, H)
        h = lax.rem(me.h + H - n, H)
        out_plane(h).wait_recv()
        load = pltpu.make_async_copy(r.out_in.at[h], r.stage.at[h], r.own_sem.at[12])
        load.start()

        def weigh(p):
            g = r.gate_all[h, pl.ds(z.expert(me, p), 1), :] * r.pick[h, p].astype(jnp.float32)
            high = g.astype(jnp.bfloat16)
            r.mix_hi[p] = high
            r.mix_lo[p] = (g - high.astype(jnp.float32)).astype(jnp.bfloat16)
        times(P, weigh)
        load.wait()
        rows = r.stage[h].reshape(P * CAP, D)
        total = tn(r.mix_hi[...].reshape(P * CAP, R), rows) + tn(r.mix_lo[...].reshape(P * CAP, R), rows)
        r.part_stage[h] = total.astype(jnp.bfloat16)
        @pl.when(n > 0)
        def _():
            mix_lane.start_one(H - n)
        @pl.when(n == 0)
        def _():
            r.grad_tokens[...] = total
    times(H, mix)

    def weights(d):
        part = pl.ds(pl.multiple_of(d * 256, 256), 256)
        total = tn(r.h1[:, part], r.d_qkv[...])
        r.gc_stage[part, :] = total.astype(jnp.bfloat16)
        gain = jnp.sum(total * r.wc_v[part, :].astype(jnp.float32), axis=-1, keepdims=True)
        gain = gain / r.small_v[part, EXPERTS : EXPERTS + 1].astype(jnp.float32)
        r.g_small[part, :] = jnp.where(lane_of((256, LANES)) == EXPERTS, gain, r.g_small[part, :])
    times(D // 256, weights)
    times(C, lambda c: gc_column(c).start())
    r.gs_stage[...] = (r.g_small[...] + r.gain_v[...].T).astype(jnp.bfloat16)
    times(C, lambda c: gs_column(c).start())
    own_last = [
        pltpu.make_async_copy(rows_at(stage, c * F + me.f, rs), landing.at[me.f, c], r.own_cols.at[i, c])
        for i, (stage, landing) in enumerate([(r.gc_stage, r.gc_x), (r.gs_stage, r.gs_x)]) for c in range(C)
    ]
    for copy in own_last:
        copy.start()
    for bulk in grad_lanes[3:]:
        bulk.start()
    r.go_stage[...] = tn(r.att_f[...].astype(jnp.bfloat16), r.blocks[...].reshape(L, D)).astype(jnp.bfloat16)
    go_lane.start()
    own_go = pltpu.make_async_copy(rows_at(r.go_stage, me.f, rs), r.go_in.at[me.f], r.own_sem.at[13])
    own_go.start()
    for copy in own_last:
        copy.wait()
    times(C, lambda c: gc_column(c).wait_recv())
    times(C, lambda c: gs_column(c).wait_recv())
    gc_total = r.gc_x[0].astype(jnp.float32)
    gs_total = r.gs_x[0].astype(jnp.float32)
    for f in range(1, F):
        gc_total = gc_total + r.gc_x[f].astype(jnp.float32)
        gs_total = gs_total + r.gs_x[f].astype(jnp.float32)
    r.gc_sum[...] = gc_total.astype(jnp.bfloat16)
    r.gs_sum[...] = gs_total.astype(jnp.bfloat16)
    gc_lane.start()
    gs_lane.start()
    own_sums = [
        pltpu.make_async_copy(r.gc_sum.at[me.c], r.gc_in.at[me.c], r.own_sem.at[14]),
        pltpu.make_async_copy(r.gs_sum.at[me.c], r.gs_in.at[me.c], r.own_sem.at[15]),
    ]
    for copy in own_sums:
        copy.start()
    mix_lane.wait_recv()

    def add_mix(n):
        r.grad_tokens[...] += r.mix_in[lax.rem(me.h + n + 1, H)].astype(jnp.float32)
    times(H - 1, add_mix)
    r.output[...] = (r.middle[...] + residual_scale * r.grad_tokens[...]).astype(jnp.bfloat16)

    dn_lane.wait_recv()
    d_h1 = dn_in(0)[...].astype(jnp.float32)
    for c in range(1, J):
        d_h1 = d_h1 + dn_in(c)[...].astype(jnp.float32)
    x = r.tok[...].astype(jnp.float32)
    inverse = lax.rsqrt(jnp.mean(x * x, axis=-1, keepdims=True) + norm_eps)
    n1 = x * inverse
    g = d_h1 * gain_one
    r.grad_tokens[...] = r.d_mid[...] + inverse * (g - n1 * jnp.mean(g * n1, axis=-1, keepdims=True))
    for last in [gc_lane, gs_lane, go_lane]:
        last.wait_recv()
    for last in grad_lanes:
        last.wait_recv()
    for last in [tok_lane, place_lane, wc_lane, small_lane, wo_lane, cot_lane, slot_lane, gate_a_lane, gate_b_lane, up_lane,
                 down_lane, att_lane, rows_lane, gates_lane, turn_lane, up_attn_lane, mix_lane, dn_lane, gc_lane,
                 gs_lane, go_lane] + grad_lanes:
        last.wait_send()
    for last in [wo_relay, up_attn_relay]:
        last.wait_send()
    times(J, lambda j: sib_copy(j).wait_send())
    for last in [g_plane, back_plane, dg_plane, out_plane]:
        times(H, lambda h, last=last: last(h).wait_send())
    for last in [wc_column, small_column, wo_column, gc_column, gs_column]:
        times(C, lambda c, last=last: last(c).wait_send())
    for copy in own_grads + own_sums + [own_go]:
        copy.wait()


def layer_call(z, R, ff, dc, tok, place, routes, cot, w_pack, small, w_out, w_gate, w_up, w_downt):
    C, F, N, H, P, J, S, rs = z.C, z.F, z.N, z.H, z.P, z.J, z.S, z.rows_w
    L, f, f16 = C * R, jnp.float32, jnp.bfloat16
    rows, heads, tile = H * P * CAP, z.q_heads * R, 8 * CAP
    ins = dict(tok=(tok, 1), place=(place, 1), routes=(routes, 1), cot=(cot, 1), freq=(frequencies(), 1), w_pack=(w_pack, 0),
               small=(small, 0), w_out=(w_out, 0), w_gate=(w_gate, 0), w_up=(w_up, 0), w_downt=(w_downt, 0))
    outs = dict(
        output=(shape_of((R, D)), 1), grad_tokens=(shape_of((R, D), f), 1), gc_in=(shape_of((C, rs, 2 * LANES)), 0),
        gs_in=(shape_of((C, rs, LANES)), 0), go_in=(shape_of((F, rs, D)), 0), gw_in=(shape_of((3, S, z.G, dc, ff)), 0),
        out_in=(shape_of((H, P, CAP, D)), 0))
    scratch = dict(
        blocks=vmem((C, R, D)), place_all=vmem((C, 8, R), jnp.int32), wc_v=vmem((D, 2 * LANES)), small_v=vmem((D, LANES)),
        wo_v=vmem((D, D)), cot_all=vmem((H, R, D)), slot_all=vmem((H, EXPERTS, R), f), slot_t=vmem((LANES, R), f),
        place_col=vmem((L, R), f), place_row=vmem((C, 8, R), f), h1=vmem((L, D)), q_all=vmem((L, LANES)), k2=vmem((L, LANES)),
        v2=vmem((L, LANES)), lse=vmem((z.q_heads, L, LANES), f), att_f=vmem((L, LANES), f), att_stage=vmem((C, R, LANES)),
        att_in=vmem((C, R, LANES)), middle=vmem((R, D), f), h2=vmem((R, D)), gates_t=vmem((LANES, R), f),
        gate_all=vmem((H, EXPERTS, R), f), h_all=vmem((H, R, D)), pick=vmem((H, P, CAP, R)), stage=vmem((H, P, CAP, D)),
        xin=vmem((rows, D)), g_stage=vmem((H, P, 8, LANES), f), gin=vmem((H, P, 8, LANES), f), wv=vmem((3, C, dc, ff)),
        cot_v=vmem((rows, D)), d_rows=vmem((H, P, CAP, D)), dg_stage=vmem((H, P, 8, LANES), f),
        dg_in=vmem((H, P, 8, LANES), f), hid=vmem((rows, ff)), d_gate=vmem((rows, ff)), d_up=vmem((rows, ff)),
        pool=vmem((max(rows, L), D)), g_col=vmem((tile, LANES), f), result=vmem((H, P, CAP, D)),
        part_stage=vmem((H, R, D)), part_in=vmem((H, R, D)), turn_stage=vmem((H, EXPERTS, R), f),
        turn_in=vmem((H, EXPERTS, R), f), turn_v=vmem((LANES, R), f), d_mid=vmem((R, D), f), d_attn=vmem((R, D)),
        g_small=vmem((D, LANES), f), gain_v=vmem((LANES, D), f), ds_v=vmem((heads, L)), p_v=vmem((heads, L)),
        q_v=vmem((heads, LANES)), dm_v=vmem((heads, LANES)), dk_acc=vmem((L, LANES), f), dv_acc=vmem((L, LANES), f),
        d_qkv=vmem((L, 2 * LANES)),
        gc_stage=vmem((D, 2 * LANES)), go_stage=vmem((LANES, D)), gs_stage=vmem((D, LANES)), gc_x=vmem((F, C, rs, 2 * LANES)),
        gs_x=vmem((F, C, rs, LANES)), gc_sum=vmem((C, rs, 2 * LANES)), gs_sum=vmem((C, rs, LANES)), mix_hi=vmem((P, CAP, R)),
        mix_lo=vmem((P, CAP, R)), mix_in=vmem((H, R, D)), own_sem=pltpu.SemaphoreType.DMA((16,)),
        own_cols=pltpu.SemaphoreType.DMA((2, C)))
    both = ("_send", "_recv")
    scratch |= {"lane_" + n + b: pltpu.SemaphoreType.DMA((z.count(g),)) for n, g in LANE_GROUPS.items() for b in both}
    scratch |= {"plane_" + n + b: pltpu.SemaphoreType.DMA((H, P)) for n in PLANE_LANES for b in both}
    scratch |= {"column_" + n + b: pltpu.SemaphoreType.DMA((C, F)) for n in COLUMN_LANES for b in both}
    scratch |= {"relay_" + n + b: pltpu.SemaphoreType.DMA((J,)) for n in RELAYS for b in both}
    names = list(ins) + list(outs) + list(scratch)
    space = lambda fast: pl.BlockSpec(memory_space=pltpu.VMEM if fast else pl.ANY)
    results = pl.pallas_call(
        functools.partial(layer_kernel, z, R, dc, tile, names), name="layer",
        out_shape=[o for o, _ in outs.values()], in_specs=[space(fast) for _, fast in ins.values()],
        out_specs=[space(fast) for _, fast in outs.values()], scratch_shapes=list(scratch.values()),
        compiler_params=pltpu.CompilerParams(collective_id=0, has_side_effects=True, vmem_limit_bytes=67043328),
    )(*[a for a, _ in ins.values()])
    return results[:6]


def local(z, tokens, norm_first, w_query, w_key, w_value, w_out, norm_second, w_router,
          w_gate, w_up, w_down, positions, routes, cotangent):
    C, F = z.C, z.F
    R = tokens.shape[1]
    rs = z.rows_w
    ff = w_gate.shape[2]
    dc = D // C

    heads_q = jnp.pad(w_query.reshape(rs, C, z.q_width), ((0, 0), (0, 0), (0, LANES - z.q_width)))
    heads_k = jnp.repeat(w_key.reshape(rs, KV_HEADS, HEAD), z.share, axis=1)
    heads_v = jnp.repeat(w_value.reshape(rs, KV_HEADS, HEAD), z.share, axis=1)
    w_pack = jnp.concatenate([heads_q, heads_k, heads_v], axis=2).transpose(1, 0, 2)
    small = jnp.concatenate(
        [w_router, norm_first[:, None], norm_second[:, None], jnp.zeros((rs, 128 - EXPERTS - 2), jnp.bfloat16)], axis=1)
    place_pack = jnp.broadcast_to(positions[0][None, :], (8, R))
    w_downt = w_down.transpose(0, 2, 1)
    output, grad_tokens, gc_in, gs_in, go_in, gw_in = layer_call(
        z, R, ff, dc, tokens[0], place_pack, routes[0], cotangent[0], w_pack, small, w_out, w_gate, w_up, w_downt)
    gc = f32(gc_in)
    join = lambda a: a.reshape(KV_HEADS, z.share, rs, HEAD).sum(axis=1).transpose(1, 0, 2).reshape(rs, KV_HEADS * HEAD)
    gs = jnp.sum(f32(gs_in), axis=0)
    return (
        output[None],
        grad_tokens[None],
        gs[:, EXPERTS],
        gc[:, :, : z.q_width].transpose(1, 0, 2).reshape(rs, D),
        join(gc[:, :, LANES : LANES + HEAD]),
        join(gc[:, :, LANES + HEAD :]),
        jnp.sum(f32(go_in), axis=0),
        gs[:, EXPERTS + 1],
        gs[:, :EXPERTS],
        jnp.sum(f32(gw_in[0]), axis=0),
        jnp.sum(f32(gw_in[1]), axis=0),
        jnp.sum(f32(gw_in[2]), axis=0).transpose(0, 2, 1),
    )


def solution(mesh):
    row = P(("ctx", "fsdp"), None)
    vec = P(("ctx", "fsdp"))
    seq = P("fsdp", "ctx", None)
    down = P("fsdp", None, "ctx")
    return jax.shard_map(
        functools.partial(local, Sizes(mesh)),
        mesh=mesh,
        in_specs=(seq, vec, row, row, row, row, vec, row, seq, seq, down, P("fsdp", "ctx"), seq, seq),
        out_specs=(seq, seq, vec, row, row, row, row, vec, row, seq, seq, down),
        check_vma=False,
    )
```

profile of v0, /device:TPU:9, one launch (start us, length us, event | category | flops | bytes accessed | tf_op | source)
XLA Modules:
  0.0 387.4 jit_solution(17964962915762061968)
XLA Ops:
  0.7 0.1 pad.3.clone
  0.7 1.2 broadcast_in_dim.23.refs_1_
  2.0 0.7 copy.36
  2.7 0.8 copy.37
  3.5 1.4 maximum_maximum_fusion.refs_6_
  4.9 0.9 copy_bitcast_fusion.1
  5.7 0.9 reshape_broadcast_in_dim_reshape.6
  6.6 0.9 reshape_broadcast_in_dim_reshape.7
  7.5 0.7 maximum_bitcast_fusion.refs_5_
  8.2 1.4 copy.32
  9.7 2.3 copy.38
  11.9 360.8 %layer.1 = (bf16[128,1024]{1,0:T(8,128)(2,1)}, f32[128,1024]{1,0:T(8,128)}, bf16[8,32,256]{2,1,0:T(8,128)(2,1)}, bf16[8,32,128]{2,1,0:T(8,128)(2,1)}, bf16[4,32,...) custom-call(bf16[128,1024]{1,0:T(8,128)(2,1)} %bitcast.42, ...), custom_call_target="tpu_custom_call" | custom-call | tf_op jit(solution)/shard_map/layer/pallas_call | solution.py:832
  372.8 0.9 convert_reduce_fusion.1
  373.6 0.0 copy-start.2
  373.6 0.7 slice_reduce_fusion
  374.3 1.7 convert_reduce_fusion
  376.0 0.9 convert_element_type.35
  376.9 0.7 copy_bitcast_fusion
  377.6 0.1 slice_bitcast_fusion
  377.7 0.1 copy.41
  377.8 0.7 reshape.66
  378.5 0.1 copy.40
  378.6 0.7 reshape.65
  379.3 4.8 %convert_bitcast_fusion = (f32[8,512,128]{1,2,0:T(8,128)S(1)}, f32[8,128,512]{2,1,0:T(8,128)}, f32[8,128,512]{2,1,0:T(8,128)}) fusion(bf16[3,1,8,128,512]{4,3,2,1,0:T(8,128)(2,1)} %get-tuple-element.23), kind=kLoop, calls=%fused_computation | loop fusion | flops 1572864 | bytes 9437184 | tf_op jit(solution)/shard_map/transpose | solution.py:874
  384.0 0.0 copy-done.2
  384.1 0.0 copy-start.1
  384.1 0.0 copy-start
  384.1 1.8 copy.42
  385.9 0.0 copy-done.1
  385.9 0.7 copy.49
  386.6 0.0 copy-done
  386.6 0.8 copy.50
  (3 shorter events, 0.0 us)
Async XLA Ops:
  373.6 10.4 %copy-start.2 = (f32[32,128]{1,0:T(8,128)}, f32[32,128]{1,0:T(8,128)S(1)}, u32[]{:S(2)}) copy-start(f32[32,128]{1,0:T(8,128)S(1)} %convert_reduce_fusion.1) | copy-start | bytes 49156
  384.1 1.8 copy-start.1
  384.1 2.5 copy-start
where the time goes:
time: 391 us; the launch traced here: 387 us
  Pallas kernels  361 us (92%)
  local copies, waits for them, and re-layouts  15.5 us (4%)
  other arithmetic  10.3 us (3%)
    pallas_call x1, Pallas kernels, layer_call(): pl.pallas_call(functools.partial(layer_kernel, z, R, dc, tile, names), na...  361 us

commit v1 on v0

--- a/solution.py
+++ b/solution.py
@@ -123,36 +123,98 @@
         self.each(self.wait_send_one)
 
 
+class Chain:
+    def __init__(self, sizes, me, group, own, landing, sends, recvs):
+        self.col = group == "col"
+        self.place, self.n = (me.h, sizes.H) if self.col else (lax.div(me.c, 2), sizes.J)
+        self.sizes, self.me, self.own, self.landing, self.sends, self.recvs = sizes, me, own, landing, sends, recvs
+
+    def copy(self, t, to, source, landing):
+        c = self.me.s * self.sizes.G + 2 * to + self.me.k if self.col else 2 * to + self.me.k
+        return pltpu.make_async_remote_copy(
+            src_ref=source, dst_ref=landing, send_sem=self.sends.at[t], recv_sem=self.recvs.at[t],
+            device_id=(c, self.me.f), device_id_type=MESH)
+
+    def inside(self, place):
+        return jnp.logical_and(place >= 0, place < self.n)
+
+    def origin(self, t):
+        return self.place - (1 - 2 * lax.rem(t, 2)) * (lax.div(t, 2) + 1)
+
+    def start(self):
+        for t, to in ((0, self.place + 1), (1, self.place - 1)):
+            @pl.when(self.inside(to))
+            def _(t=t, to=to):
+                self.copy(t, to, self.own, self.landing(self.place)).start()
+
+    def take(self, t):
+        sign = 1 - 2 * lax.rem(t, 2)
+        here = self.landing(self.origin(t))
+        self.copy(t, self.place - sign, here, here).wait_recv()
+        @pl.when(self.inside(self.place + sign))
+        def _():
+            self.copy(t + 2, self.place + sign, here, here).start()
+
+    def wait_send(self):
+        def one(t, carry):
+            to = self.place + 1 - 2 * lax.rem(t, 2)
+            origin = to - (1 - 2 * lax.rem(t, 2)) * (lax.div(t, 2) + 1)
+            @pl.when(jnp.logical_and(self.inside(to), self.inside(origin)))
+            def _():
+                self.copy(t, to, self.landing(self.place), self.landing(self.place)).wait_send()
+            return carry
+        lax.fori_loop(0, 2 * (self.n - 1), one, 0)
+
+    def visit(self, step, relay=None):
+        each = 2 * self.n - 1
+
+        def one(i):
+            u = lax.rem(i, each)
+            origin = jnp.where(u == 0, self.place, self.origin(jnp.maximum(u - 1, 0)))
+            @pl.when(self.inside(origin))
+            def _():
+                @pl.when(jnp.logical_and(u > 0, i < each))
+                def _():
+                    self.take(u - 1)
+                    if relay is not None:
+                        relay.start(origin)
+                if relay is None:
+                    step(origin)
+                else:
+                    @pl.when(i >= each)
+                    def _():
+                        relay.wait_recv(origin)
+                    step(origin, jnp.where(i < each, self.me.k, 1 - self.me.k))
+        times(each if relay is None else 2 * each, one)
+
+
 class Relay:
     def __init__(self, sizes, me, own, landing, sends, recvs):
-        self.sizes, self.me, self.own, self.landing, self.sends, self.recvs = sizes, me, own, landing, sends, recvs
-
-    def member(self, n, core):
-        J = self.sizes.J
-        return 2 * lax.rem(lax.div(self.me.c, 2) + J - n, J) + core
-
-    def copy(self, n, source, landing):
+        self.J, self.me, self.own, self.landing, self.sends, self.recvs = sizes.J, me, own, landing, sends, recvs
+        self.place = lax.div(me.c, 2)
+
+    def copy(self, place, source, landing):
         return pltpu.make_async_remote_copy(
-            src_ref=source, dst_ref=landing, send_sem=self.sends.at[n], recv_sem=self.recvs.at[n],
+            src_ref=source, dst_ref=landing, send_sem=self.sends.at[place], recv_sem=self.recvs.at[place],
             device_id=(self.me.c + 1 - 2 * self.me.k, self.me.f), device_id_type=MESH)
 
     def start_own(self):
-        self.copy(0, self.own, self.landing(self.me.c)).start()
-
-    def start_one(self, n):
-        here = self.landing(self.member(n, self.me.k))
-        self.copy(n, here, here).start()
-
-    def wait_recv_one(self, n):
-        there = self.landing(self.member(n, 1 - self.me.k))
-        self.copy(n, there, there).wait_recv()
+        self.copy(self.place, self.own, self.landing(self.me.c)).start()
+
+    def start(self, place):
+        here = self.landing(2 * place + self.me.k)
+        self.copy(place, here, here).start()
+
+    def wait_recv(self, place):
+        there = self.landing(2 * place + 1 - self.me.k)
+        self.copy(place, there, there).wait_recv()
 
     def wait_send(self):
-        def one(n, carry):
-            here = self.landing(self.member(n, self.me.k))
-            self.copy(n, here, here).wait_send()
+        def one(place, carry):
+            here = self.landing(2 * place + self.me.k)
+            self.copy(place, here, here).wait_send()
             return carry
-        lax.fori_loop(0, self.sizes.J, one, 0)
+        lax.fori_loop(0, self.J, one, 0)
 
 
 def meet(sizes, me, groups):
@@ -225,9 +287,10 @@
     return lax.dot_general(a, b, (dims, ((), ())), precision=lax.Precision.HIGHEST, preferred_element_type=jnp.float32)
 
 
+CHAIN_GROUPS = dict(tok="line", wo="line", cot="col", rows="col", d_attn="line")
 LANE_GROUPS = dict(
-    tok="line", place="ctx", wc="ctx", small="ctx", wo="line", cot="col", slot="col", gate_a="ctx", gate_b="ctx", up="ctx",
-    down="ctx", att="ctx", rows="col", gates="col", part="col", turn="col", d_attn="line", mix="col", dn="line", gc="ctx",
+    place="ctx", wc="ctx", small="ctx", slot="col", gate_a="ctx", gate_b="ctx", up="ctx",
+    down="ctx", att="ctx", gates="col", part="col", turn="col", mix="col", dn="line", gc="ctx",
     gs="ctx", go="fsdp", grad0="ctx", grad1="ctx", grad2="ctx", grad3="ctx", grad4="ctx", grad5="ctx")
 PLANE_LANES = ["cot", "row", "g", "back", "dg", "out"]
 COLUMN_LANES = ["wc", "small", "wo", "gc", "gs"]
@@ -249,6 +312,9 @@
     def lane(name, source, landing):
         return Lane(z, me, LANE_GROUPS[name], source, landing, *sems("lane_", name))
 
+    def chain(name, own, landing):
+        return Chain(z, me, CHAIN_GROUPS[name], own, landing, *sems("chain_", name))
+
     def plane(name, source, landing):
         def at(h):
             send, recv = sems("plane_", name)
@@ -262,28 +328,28 @@
     def relay(name, own, landing):
         return Relay(z, me, own, landing, *sems("relay_", name))
 
-    tok_lane = lane("tok", lambda to: r.tok, lambda p: r.blocks.at[p.c])
+    tok_chain = chain("tok", r.tok, lambda place: r.blocks.at[2 * place + me.k])
     tok_relay = relay("tok", r.tok, lambda c: r.blocks.at[c])
     place_lane = lane("place", lambda to: r.place, lambda p: r.place_all.at[p.c])
     wc_lane = lane("wc", lambda to: r.w_pack.at[to.c], lambda p: rows_at(r.wc_v, p.w, rs))
     small_lane = lane("small", lambda to: r.small, lambda p: rows_at(r.small_v, p.w, rs))
-    wo_lane = lane("wo", lambda to: r.w_out, lambda p: rows_at(r.wo_v, p.w, rs))
+    wo_chain = chain("wo", r.w_out, lambda place: rows_at(r.wo_v, (2 * place + me.k) * F + me.f, rs))
     wo_relay = relay("wo", r.w_out, lambda c: rows_at(r.wo_v, c * F + me.f, rs))
     spread = lambda name, ref: column(
         name, lambda c, to: rows_at(ref, c * F + me.f, rs), lambda c, p: rows_at(ref, c * F + p.f, rs))
     wc_column, small_column, wo_column = spread("wc", r.wc_v), spread("small", r.small_v), spread("wo", r.wo_v)
-    cot_lane = lane("cot", lambda to: r.cot, lambda p: r.cot_all.at[p.h])
+    cot_chain = chain("cot", r.cot, lambda h: r.cot_all.at[h])
     slot_lane = lane("slot", lambda to: r.slot_t.at[pl.ds(0, EXPERTS), :], lambda p: r.slot_all.at[p.h])
     gate_a_lane = lane("gate_a", lambda to: r.w_gate.at[to.m, low], lambda p: r.wv.at[0, p.c, low])
     gate_b_lane = lane("gate_b", lambda to: r.w_gate.at[to.m, high], lambda p: r.wv.at[0, p.c, high])
     up_lane = lane("up", lambda to: r.w_up.at[to.m], lambda p: r.wv.at[1, p.c])
     down_lane = lane("down", lambda to: r.w_downt.at[to.m], lambda p: r.wv.at[2, p.c])
     att_lane = lane("att", lambda to: r.att_stage.at[to.c], lambda p: r.att_in.at[p.c])
-    rows_lane = lane("rows", lambda to: r.h2, lambda p: r.h_all.at[p.h])
+    rows_chain = chain("rows", r.h2, lambda h: r.h_all.at[h])
     gates_lane = lane("gates", lambda to: r.gates_t.at[pl.ds(0, EXPERTS), :], lambda p: r.gate_all.at[p.h])
     part_lane = lane("part", lambda to: r.part_stage.at[to.h], lambda p: r.part_in.at[p.h])
     turn_lane = lane("turn", lambda to: r.turn_stage.at[to.h], lambda p: r.turn_in.at[p.h])
-    up_attn_lane = lane("d_attn", lambda to: r.d_attn, lambda p: r.blocks.at[p.c])
+    up_attn_chain = chain("d_attn", r.d_attn, lambda place: r.blocks.at[2 * place + me.k])
     up_attn_relay = relay("d_attn", r.d_attn, lambda c: r.blocks.at[c])
     mix_lane = lane("mix", lambda to: r.part_stage.at[to.h], lambda p: r.mix_in.at[p.h])
     dn_block = lambda c: rows_at(r.pool, c, R)
@@ -296,9 +362,10 @@
     gather = lambda name, stage, landing: column(
         name, lambda c, to: rows_at(stage, c * F + to.f, rs), lambda c, p: landing.at[p.f, c])
     gc_column, gs_column = gather("gc", r.gc_stage, r.gc_x), gather("gs", r.gs_stage, r.gs_x)
+    grad_of = lambda j, c: rows_at(r.g_down, c, dc) if j == 2 else r.wv.at[j, c]
     grad_lanes = [
         lane("grad" + str(2 * j + i),
-             lambda to, j=j, i=i: r.wv.at[j, to.c, (low, high)[i]],
+             lambda to, j=j, i=i: grad_of(j, to.c).at[(low, high)[i]],
              lambda p, j=j, i=i: r.gw_in.at[j, p.s, p.m, (low, high)[i]])
         for j in range(3) for i in range(2)
     ]
@@ -319,8 +386,6 @@
     wc_lane.start()
     small_lane.start()
     place_lane.start()
-    tok_relay.start_own()
-    tok_lane.start()
 
     own = [
         pltpu.make_async_copy(r.w_pack.at[me.c], rows_at(r.wc_v, me.w, rs), r.own_sem.at[0]),
@@ -348,49 +413,49 @@
     slot_lane.start()
     slot_id = lax.broadcasted_iota(jnp.int32, (CAP, R), 0).astype(jnp.float32)
 
+    wc_lane.wait_recv()
+    small_lane.wait_recv()
+    wo_relay.start_own()
+    wo_chain.start()
+    tok_relay.start_own()
+    tok_chain.start()
+    cot_chain.start()
     for copy in own:
         copy.wait()
-    wc_lane.wait_recv()
     times(C, lambda c: wc_column(c).start())
-    small_lane.wait_recv()
     times(C, lambda c: small_column(c).start())
 
-    def dispatch_cot(j):
+    def choose(j):
         h = lax.rem(me.h + H - j, H)
         @pl.when(j > 0)
         def _():
-            cot_lane.wait_recv_one(j)
             slot_lane.wait_recv_one(j)
 
+        def for_expert(p):
+            row = r.slot_all[h, pl.ds(z.expert(me, p), 1), :]
+            r.pick[h, p] = jnp.where(row == slot_id, 1.0, 0.0).astype(jnp.bfloat16)
+        times(P, for_expert)
+
+    def dispatch_cot(h):
         def to_expert(n):
             p = lax.rem(me.p + n, P)
-            row = r.slot_all[h, pl.ds(z.expert(me, p), 1), :]
-            hot = jnp.where(row == slot_id, 1.0, 0.0).astype(jnp.bfloat16)
-            r.pick[h, p] = hot
-            r.d_rows[h, p] = nn(hot, r.cot_all[h]).astype(jnp.bfloat16)
+            r.d_rows[h, p] = nn(r.pick[h, p], r.cot_all[h]).astype(jnp.bfloat16)
             @pl.when(n > 0)
             def _():
                 cot_plane(h).start_one(n)
         times(P, to_expert)
         at_slot(r.cot_v, h, me.p)[...] = r.d_rows[h, me.p]
-    dispatch_cot(0)
     place_lane.wait_recv()
     times(C, lambda c: wc_column(c).wait_recv())
     times(C, lambda c: small_column(c).wait_recv())
+    times(H, choose)
+    wo_chain.visit(lambda place, core: wo_column(2 * place + core).start(), wo_relay)
     gain_one = r.small_v[...].astype(jnp.float32).T[EXPERTS : EXPERTS + 1, :]
     gain_two = r.small_v[...].astype(jnp.float32).T[EXPERTS + 1 : EXPERTS + 2, :]
     head_of = lax.div(lane_of((R, LANES)), HEAD)
 
-    def project(i):
-        n = lax.rem(i, J)
-        c = tok_relay.member(n, jnp.where(i < J, me.k, 1 - me.k))
-        @pl.when(jnp.logical_and(i > 0, i < J))
-        def _():
-            tok_lane.wait_recv_one(n)
-            tok_relay.start_one(n)
-        @pl.when(i >= J)
-        def _():
-            tok_relay.wait_recv_one(n)
+    def project(place, core):
+        c = 2 * place + core
         x = r.blocks[c].astype(jnp.float32)
         inverse = lax.rsqrt(jnp.mean(x * x, axis=-1, keepdims=True) + norm_eps)
         h = (x * inverse * gain_one).astype(jnp.bfloat16)
@@ -406,10 +471,8 @@
         swapped = pltpu.roll(kv, HEAD, 1)
         r.k2[part, :] = jnp.where(head_of == 0, kv, swapped).astype(jnp.bfloat16)
         r.v2[part, :] = jnp.where(head_of == 0, swapped, kv).astype(jnp.bfloat16)
-    times(C, project)
-    wo_relay.start_own()
-    wo_lane.start()
-    cot_lane.start()
+    tok_chain.visit(project, tok_relay)
+    gate_a_lane.start()
     tok_relay.wait_send()
 
     def attend(c):
@@ -429,16 +492,11 @@
             total = jnp.where(mine, nn(e.astype(jnp.bfloat16), r.v2[...]) / weight, total)
         r.att_f[part, :] = total
         r.att_stage[c] = total.astype(jnp.bfloat16)
-    times(C // 2, attend)
-    wo_lane.wait_recv()
-    times(J, wo_relay.start_one, 1)
-    times(C, attend, C // 2)
+    times(C, attend)
+    tok_chain.wait_send()
     att_lane.start()
-    gate_a_lane.start()
     r.att_in[me.c] = r.att_stage[me.c]
-    times(J, wo_relay.wait_recv_one)
-    times(C, lambda c: wo_column(c).start())
-    times(H, dispatch_cot, 1)
+    cot_chain.visit(dispatch_cot)
     att_lane.wait_recv()
     times(C, lambda c: wo_column(c).wait_recv())
     x = r.tok[...].astype(jnp.float32)
@@ -450,24 +508,19 @@
     inverse = lax.rsqrt(jnp.mean(mid * mid, axis=-1, keepdims=True) + norm_eps)
     hidden = (mid * inverse * gain_two).astype(jnp.bfloat16)
     r.h2[...] = hidden
-    rows_lane.start()
+    rows_chain.start()
     chosen = r.slot_t[...].T > -0.5
     logits = jnp.where(chosen, nn(hidden, r.small_v[...]), masked_score)
     raised = jnp.where(chosen, jnp.exp(logits - jnp.max(logits, axis=-1, keepdims=True)), 0.0)
     r.gates_t[...] = (raised / jnp.sum(raised, axis=-1, keepdims=True)).T
     gates_lane.start()
-    gate_b_lane.start()
-    up_lane.start()
-    down_lane.start()
     r.h_all[me.h] = r.h2[...]
     r.gate_all[me.h] = r.gates_t[0:EXPERTS, :]
 
-    def dispatch_rows(j):
-        h = lax.rem(me.h + H - j, H)
-        @pl.when(j > 0)
+    def dispatch_rows(h):
+        @pl.when(h != me.h)
         def _():
-            rows_lane.wait_recv_one(j)
-            gates_lane.wait_recv_one(j)
+            gates_lane.wait_recv_one(lax.rem(me.h + H - h, H))
 
         def to_expert(n):
             p = lax.rem(me.p + n, P)
@@ -482,7 +535,10 @@
         times(P, to_expert)
         at_slot(r.xin, h, me.p)[...] = r.stage[h, me.p]
         r.gin[h, me.p] = r.g_stage[h, me.p]
-    times(H, dispatch_rows)
+    rows_chain.visit(dispatch_rows)
+    gate_b_lane.start()
+    up_lane.start()
+    down_lane.start()
 
     def send_gates(j):
         h = lax.rem(me.h + H - j, H)
@@ -495,37 +551,52 @@
     times(H, lambda h: cot_plane(h).wait_send())
     for copy in own_weights:
         copy.wait()
-    for bulk in [gate_a_lane, gate_b_lane, up_lane, down_lane]:
+    for bulk in [gate_a_lane, gate_b_lane, up_lane]:
         bulk.wait_recv()
     times(H, lambda h: cot_plane(h).wait_recv())
     wg, wu, wd = [r.wv.at[j].reshape(D, r.wv.shape[3]) for j in range(3)]
     per = tile // CAP
 
-    def chunk(j):
+    def forward(j):
         h = lax.rem(me.h + H - lax.rem(j + 1, H), H)
         row_plane(h).wait_recv()
         g_plane(h).wait_recv()
 
         def rows(t):
-            some = pl.ds(pl.multiple_of(t * per, per), per)
             part = pl.ds(pl.multiple_of((h * P + t * per) * CAP, CAP), tile)
             for p in range(per):
                 turned = jnp.broadcast_to(r.gin[h, t * per + p, 0:1, :], (LANES, LANES)).T
                 r.g_col[p * CAP : (p + 1) * CAP, :] = turned[0:CAP, :]
             x = r.xin[part, :]
+            r.hid[part, :] = (jax.nn.silu(nn(x, wg[...])) * nn(x, wu[...])).astype(jnp.bfloat16)
+            r.pool[part, :] = (residual_scale * r.g_col[:, 0:1] * r.cot_v[part, :].astype(jnp.float32)).astype(jnp.bfloat16)
+        times(P // per, rows)
+    times(H, forward)
+
+    def cut_down(d):
+        part = pl.ds(pl.multiple_of(d * 256, 256), 256)
+        r.g_down[part, :] = tn(r.pool[pl.ds(0, H * P * CAP), part], r.hid[...]).astype(jnp.bfloat16)
+    times(D // 256, cut_down)
+    grad_lanes[4].start()
+    grad_lanes[5].start()
+    down_lane.wait_recv()
+
+    def chunk(j):
+        h = lax.rem(me.h + H - lax.rem(j + 1, H), H)
+
+        def rows(t):
+            some = pl.ds(pl.multiple_of(t * per, per), per)
+            part = pl.ds(pl.multiple_of((h * P + t * per) * CAP, CAP), tile)
+            x = r.xin[part, :]
             gate = nn(x, wg[...])
             up = nn(x, wu[...])
             sig = jax.nn.sigmoid(gate)
             act = gate * sig
-            hidden = (act * up).astype(jnp.bfloat16)
-            r.hid[part, :] = hidden
-            out = nt(hidden, wd[...]).astype(jnp.bfloat16)
+            out = nt(r.hid[part, :], wd[...]).astype(jnp.bfloat16)
             r.result[h, some] = out.reshape(per, CAP, D)
             upstream = r.cot_v[part, :].astype(jnp.float32)
             d_gates = residual_scale * jnp.sum(upstream * out.astype(jnp.float32), axis=-1, keepdims=True)
-            d_out = (residual_scale * r.g_col[:, 0:1] * upstream).astype(jnp.bfloat16)
-            r.pool[part, :] = d_out
-            d_hidden = nn(d_out, wd[...])
+            d_hidden = nn(r.pool[part, :], wd[...])
             dg = (d_hidden * up * sig * (1.0 + gate * (1.0 - sig))).astype(jnp.bfloat16)
             du = (d_hidden * act).astype(jnp.bfloat16)
             r.d_gate[part, :] = dg
@@ -542,20 +613,16 @@
         r.stage[h, me.p] = r.d_rows[h, me.p]
         r.dg_in[h, me.p] = r.dg_stage[h, me.p]
     times(H, chunk)
-    times(H, lambda h: out_plane(h).start())
-    own_out = pltpu.make_async_copy(r.result.at[:, me.p], r.out_in.at[:, me.p], r.own_sem.at[7])
-    own_out.start()
 
     def cut(d):
         part = pl.ds(pl.multiple_of(d * 256, 256), 256)
         x = r.xin[:, part]
         wg[part, :] = tn(x, r.d_gate[...]).astype(jnp.bfloat16)
         wu[part, :] = tn(x, r.d_up[...]).astype(jnp.bfloat16)
-        wd[part, :] = tn(r.pool[pl.ds(0, H * P * CAP), part], r.hid[...]).astype(jnp.bfloat16)
     times(D // 256, cut)
     grad_lanes[0].start()
     own_grads = [
-        pltpu.make_async_copy(r.wv.at[j, me.c], r.gw_in.at[j, me.s, me.m], r.own_sem.at[8 + j]) for j in range(3)
+        pltpu.make_async_copy(grad_of(j, me.c), r.gw_in.at[j, me.s, me.m], r.own_sem.at[8 + j]) for j in range(3)
     ]
     for copy in own_grads:
         copy.start()
@@ -583,7 +650,9 @@
             r.turn_v[...] = jnp.zeros((LANES, R), jnp.float32)
             r.turn_v[0:EXPERTS, :] = r.turn_stage[h]
     times(H, collect)
-    grad_lanes[1].start()
+    times(H, lambda h: out_plane(h).start())
+    own_out = pltpu.make_async_copy(r.result.at[:, me.p], r.out_in.at[:, me.p], r.own_sem.at[7])
+    own_out.start()
     part_lane.wait_recv()
     turn_lane.wait_recv()
 
@@ -604,8 +673,7 @@
     r.d_mid[...] = dm
     r.d_attn[...] = (residual_scale * dm).astype(jnp.bfloat16)
     up_attn_relay.start_own()
-    up_attn_lane.start()
-    grad_lanes[2].start()
+    up_attn_chain.start()
     r.gain_v[...] = jnp.zeros((LANES, D), jnp.float32)
     r.gain_v[EXPERTS + 1 : EXPERTS + 2, :] = jnp.sum(d_h2 * n2, axis=0, keepdims=True)
     r.g_small[...] = exact("tn", r.h2[...].astype(jnp.float32), d_log)
@@ -615,16 +683,8 @@
     r.dv_acc[...] = jnp.zeros((L, LANES), jnp.float32)
     wo_c = rows_at(r.wo_v, me.c, qw)
 
-    def attend_back(i):
-        n = lax.rem(i, J)
-        c = up_attn_relay.member(n, jnp.where(i < J, me.k, 1 - me.k))
-        @pl.when(jnp.logical_and(i > 0, i < J))
-        def _():
-            up_attn_lane.wait_recv_one(n)
-            up_attn_relay.start_one(n)
-        @pl.when(i >= J)
-        def _():
-            up_attn_relay.wait_recv_one(n)
+    def attend_back(place, core):
+        c = 2 * place + core
         part = pl.ds(pl.multiple_of(c * R, R), R)
         q = r.q_all[part, :]
         d_mix = nt(r.blocks[c], wo_c[...])
@@ -653,7 +713,8 @@
         r.dv_acc[...] += tn(r.p_v[...], r.dm_v[...])
         cosine, sine = rope_tables(places, r.freq[0:1, :])
         r.d_qkv[part, 0:LANES] = rope(dq, cosine, -sine).astype(jnp.bfloat16)
-    times(C, attend_back)
+    up_attn_chain.visit(attend_back, up_attn_relay)
+    grad_lanes[1].start()
 
     def finish_kv(c):
         part = pl.ds(pl.multiple_of(c * R, R), R)
@@ -714,6 +775,8 @@
         def _():
             r.grad_tokens[...] = total
     times(H, mix)
+    grad_lanes[2].start()
+    grad_lanes[3].start()
 
     def weights(d):
         part = pl.ds(pl.multiple_of(d * 256, 256), 256)
@@ -732,8 +795,6 @@
     ]
     for copy in own_last:
         copy.start()
-    for bulk in grad_lanes[3:]:
-        bulk.start()
     r.go_stage[...] = tn(r.att_f[...].astype(jnp.bfloat16), r.blocks[...].reshape(L, D)).astype(jnp.bfloat16)
     go_lane.start()
     own_go = pltpu.make_async_copy(rows_at(r.go_stage, me.f, rs), r.go_in.at[me.f], r.own_sem.at[13])
@@ -777,9 +838,10 @@
         last.wait_recv()
     for last in grad_lanes:
         last.wait_recv()
-    for last in [tok_lane, place_lane, wc_lane, small_lane, wo_lane, cot_lane, slot_lane, gate_a_lane, gate_b_lane, up_lane,
-                 down_lane, att_lane, rows_lane, gates_lane, turn_lane, up_attn_lane, mix_lane, dn_lane, gc_lane,
-                 gs_lane, go_lane] + grad_lanes:
+    for last in [place_lane, wc_lane, small_lane, slot_lane, gate_a_lane, gate_b_lane, up_lane, down_lane, att_lane, gates_lane,
+                 turn_lane, mix_lane, dn_lane, gc_lane, gs_lane, go_lane] + grad_lanes:
+        last.wait_send()
+    for last in [wo_chain, cot_chain, rows_chain, up_attn_chain]:
         last.wait_send()
     for last in [wo_relay, up_attn_relay]:
         last.wait_send()
@@ -815,7 +877,7 @@
         pool=vmem((max(rows, L), D)), g_col=vmem((tile, LANES), f), result=vmem((H, P, CAP, D)),
         part_stage=vmem((H, R, D)), part_in=vmem((H, R, D)), turn_stage=vmem((H, EXPERTS, R), f),
         turn_in=vmem((H, EXPERTS, R), f), turn_v=vmem((LANES, R), f), d_mid=vmem((R, D), f), d_attn=vmem((R, D)),
-        g_small=vmem((D, LANES), f), gain_v=vmem((LANES, D), f), ds_v=vmem((heads, L)), p_v=vmem((heads, L)),
+        g_small=vmem((D, LANES), f), g_down=vmem((D, ff)), gain_v=vmem((LANES, D), f), ds_v=vmem((heads, L)), p_v=vmem((heads, L)),
         q_v=vmem((heads, LANES)), dm_v=vmem((heads, LANES)), dk_acc=vmem((L, LANES), f), dv_acc=vmem((L, LANES), f),
         d_qkv=vmem((L, 2 * LANES)),
         gc_stage=vmem((D, 2 * LANES)), go_stage=vmem((LANES, D)), gs_stage=vmem((D, LANES)), gc_x=vmem((F, C, rs, 2 * LANES)),
@@ -824,6 +886,8 @@
         own_cols=pltpu.SemaphoreType.DMA((2, C)))
     both = ("_send", "_recv")
     scratch |= {"lane_" + n + b: pltpu.SemaphoreType.DMA((z.count(g),)) for n, g in LANE_GROUPS.items() for b in both}
+    steps = {"col": 2 * H, "line": 2 * J}
+    scratch |= {"chain_" + n + b: pltpu.SemaphoreType.DMA((steps[g],)) for n, g in CHAIN_GROUPS.items() for b in both}
     scratch |= {"plane_" + n + b: pltpu.SemaphoreType.DMA((H, P)) for n in PLANE_LANES for b in both}
     scratch |= {"column_" + n + b: pltpu.SemaphoreType.DMA((C, F)) for n in COLUMN_LANES for b in both}
     scratch |= {"relay_" + n + b: pltpu.SemaphoreType.DMA((J,)) for n in RELAYS for b in both}

time: 391 us -> 356 us (0.910)
  Pallas kernels: 361 us -> 327 us
    pallas_call x1, Pallas kernels: 361 us -> 327 us  [layer_call(): pl.pallas_call(functools.partial(layer_kernel, z, R, dc, tile, names), na...]
where the time goes in v1:
time: 356 us; the launch traced here: 353 us
  Pallas kernels  327 us (92%)
  local copies, waits for them, and re-layouts  15.5 us (4%)
  other arithmetic  10.3 us (3%)
    pallas_call x1, Pallas kernels, layer_call(): pl.pallas_call(functools.partial(layer_kernel, z, R, dc, tile, names), na...  327 us

profile of v1, /device:TPU:9, one launch (start us, length us, event | category | flops | bytes accessed | tf_op | source)
XLA Modules:
  0.0 353.5 jit_solution(396639774171038631)
XLA Ops:
  0.7 0.1 pad.3.clone
  0.7 1.2 broadcast_in_dim.23.refs_1_
  2.0 0.7 copy.36
  2.7 0.8 copy.37
  3.5 1.4 maximum_maximum_fusion.refs_6_
  4.9 0.9 copy_bitcast_fusion.1
  5.7 0.9 reshape_broadcast_in_dim_reshape.6
  6.6 0.9 reshape_broadcast_in_dim_reshape.7
  7.5 0.7 maximum_bitcast_fusion.refs_5_
  8.2 1.4 copy.32
  9.7 2.3 copy.38
  11.9 326.9 %layer.1 = (bf16[128,1024]{1,0:T(8,128)(2,1)}, f32[128,1024]{1,0:T(8,128)}, bf16[8,32,256]{2,1,0:T(8,128)(2,1)}, bf16[8,32,128]{2,1,0:T(8,128)(2,1)}, bf16[4,32,...) custom-call(bf16[128,1024]{1,0:T(8,128)(2,1)} %bitcast.42, ...), custom_call_target="tpu_custom_call" | custom-call | tf_op jit(solution)/shard_map/layer/pallas_call | solution.py:896
  338.8 0.9 convert_reduce_fusion.1
  339.7 0.0 copy-start.2
  339.7 0.7 slice_reduce_fusion
  340.4 1.7 convert_reduce_fusion
  342.1 0.9 convert_element_type.35
  343.0 0.7 copy_bitcast_fusion
  343.7 0.1 slice_bitcast_fusion
  343.8 0.1 copy.41
  343.8 0.7 reshape.66
  344.6 0.1 copy.40
  344.6 0.7 reshape.65
  345.4 4.8 %convert_bitcast_fusion = (f32[8,512,128]{1,2,0:T(8,128)S(1)}, f32[8,128,512]{2,1,0:T(8,128)}, f32[8,128,512]{2,1,0:T(8,128)}) fusion(bf16[3,1,8,128,512]{4,3,2,1,0:T(8,128)(2,1)} %get-tuple-element.23), kind=kLoop, calls=%fused_computation | loop fusion | flops 1572864 | bytes 9437184 | tf_op jit(solution)/shard_map/transpose | solution.py:938
  350.1 0.0 copy-done.2
  350.1 0.0 copy-start.1
  350.1 0.0 copy-start
  350.1 1.8 copy.42
  352.0 0.0 copy-done.1
  352.0 0.7 copy.49
  352.7 0.0 copy-done
  352.7 0.8 copy.50
  (3 shorter events, 0.0 us)
Async XLA Ops:
  339.7 10.4 %copy-start.2 = (f32[32,128]{1,0:T(8,128)}, f32[32,128]{1,0:T(8,128)S(1)}, u32[]{:S(2)}) copy-start(f32[32,128]{1,0:T(8,128)S(1)} %convert_reduce_fusion.1) | copy-start | bytes 49156
  350.1 1.8 copy-start.1
  350.1 2.5 copy-start

commit v2 on v1

--- a/solution.py
+++ b/solution.py
@@ -164,6 +164,14 @@
                 self.copy(t, to, self.landing(self.place), self.landing(self.place)).wait_send()
             return carry
         lax.fori_loop(0, 2 * (self.n - 1), one, 0)
+
+    def visit_some(self, step, first, last):
+        def one(t):
+            @pl.when(self.inside(self.origin(t)))
+            def _():
+                self.take(t)
+                step(self.origin(t))
+        times(last, one, first)
 
     def visit(self, step, relay=None):
         each = 2 * self.n - 1
@@ -188,6 +196,64 @@
         times(each if relay is None else 2 * each, one)
 
 
+class Fold(Chain):
+    def __init__(self, sizes, me, group, total, block, landing, sends, recvs):
+        super().__init__(sizes, me, group, None, landing, sends, recvs)
+        self.total, self.block = total, block
+
+    def far_first(self, step):
+        n = self.n
+        flip = 2 * self.place >= n
+        q = jnp.where(flip, n - 1 - self.place, self.place)
+
+        def one(i):
+            left = i - (n - 1 - 2 * q)
+            near = q + (1 - 2 * lax.rem(jnp.maximum(left, 0), 2)) * (q - lax.div(jnp.maximum(left, 0), 2))
+            dest = jnp.where(left < 0, n - 1 - i, near)
+            step(jnp.where(flip, n - 1 - dest, dest))
+        times(n, one)
+
+    def index(self, dest):
+        return jnp.where(dest > self.place, dest, self.n + dest)
+
+    def add(self, index, slot):
+        here = self.landing(slot)
+        self.copy(index, self.place, here, here, self.place_of_peer()).wait_recv()
+        self.total[...] += here[...].astype(jnp.float32)
+
+    def place_of_peer(self):
+        return jnp.where(self.place > 0, self.place - 1, self.place + 1)
+
+    def copy(self, index, to, source, landing, peer=None):
+        return super().copy(index, to if peer is None else peer, source, landing)
+
+    def send(self, dest):
+        up = dest > self.place
+        @pl.when(jnp.where(up, self.place > 0, self.place < self.n - 1))
+        def _():
+            self.add(self.index(dest), dest)
+        self.block(dest)[...] = self.total[...].astype(jnp.bfloat16)
+        to = jnp.where(up, self.place + 1, self.place - 1)
+        slot = jnp.where(jnp.logical_and(jnp.logical_not(up), dest == to), self.n, dest)
+        self.copy(self.index(dest), to, self.block(dest), self.landing(slot)).start()
+
+    def finish(self):
+        @pl.when(self.place > 0)
+        def _():
+            self.add(self.place, self.place)
+        @pl.when(self.place < self.n - 1)
+        def _():
+            self.add(self.n + self.place, self.n)
+
+    def wait_send(self):
+        def one(dest, carry):
+            @pl.when(dest != self.place)
+            def _():
+                self.copy(self.index(dest), self.place_of_peer(), self.block(dest), self.landing(dest)).wait_send()
+            return carry
+        lax.fori_loop(0, self.n, one, 0)
+
+
 class Relay:
     def __init__(self, sizes, me, own, landing, sends, recvs):
         self.J, self.me, self.own, self.landing, self.sends, self.recvs = sizes.J, me, own, landing, sends, recvs
@@ -287,10 +353,10 @@
     return lax.dot_general(a, b, (dims, ((), ())), precision=lax.Precision.HIGHEST, preferred_element_type=jnp.float32)
 
 
-CHAIN_GROUPS = dict(tok="line", wo="line", cot="col", rows="col", d_attn="line")
+CHAIN_GROUPS = dict(tok="line", cot="col", rows="col", d_attn="line", part="col", mix="col", dn="line")
 LANE_GROUPS = dict(
     place="ctx", wc="ctx", small="ctx", slot="col", gate_a="ctx", gate_b="ctx", up="ctx",
-    down="ctx", att="ctx", gates="col", part="col", turn="col", mix="col", dn="line", gc="ctx",
+    down="ctx", att="ctx", gates="col", turn="col", gc="ctx", wo="line",
     gs="ctx", go="fsdp", grad0="ctx", grad1="ctx", grad2="ctx", grad3="ctx", grad4="ctx", grad5="ctx")
 PLANE_LANES = ["cot", "row", "g", "back", "dg", "out"]
 COLUMN_LANES = ["wc", "small", "wo", "gc", "gs"]
@@ -333,8 +399,8 @@
     place_lane = lane("place", lambda to: r.place, lambda p: r.place_all.at[p.c])
     wc_lane = lane("wc", lambda to: r.w_pack.at[to.c], lambda p: rows_at(r.wc_v, p.w, rs))
     small_lane = lane("small", lambda to: r.small, lambda p: rows_at(r.small_v, p.w, rs))
-    wo_chain = chain("wo", r.w_out, lambda place: rows_at(r.wo_v, (2 * place + me.k) * F + me.f, rs))
-    wo_relay = relay("wo", r.w_out, lambda c: rows_at(r.wo_v, c * F + me.f, rs))
+    wo_lane = lane("wo", lambda to: r.w_out, lambda p: rows_at(r.wo_v, p.w, rs))
+    wo_relay = relay("wo", None, lambda c: rows_at(r.wo_v, c, qw))
     spread = lambda name, ref: column(
         name, lambda c, to: rows_at(ref, c * F + me.f, rs), lambda c, p: rows_at(ref, c * F + p.f, rs))
     wc_column, small_column, wo_column = spread("wc", r.wc_v), spread("small", r.small_v), spread("wo", r.wo_v)
@@ -347,15 +413,16 @@
     att_lane = lane("att", lambda to: r.att_stage.at[to.c], lambda p: r.att_in.at[p.c])
     rows_chain = chain("rows", r.h2, lambda h: r.h_all.at[h])
     gates_lane = lane("gates", lambda to: r.gates_t.at[pl.ds(0, EXPERTS), :], lambda p: r.gate_all.at[p.h])
-    part_lane = lane("part", lambda to: r.part_stage.at[to.h], lambda p: r.part_in.at[p.h])
     turn_lane = lane("turn", lambda to: r.turn_stage.at[to.h], lambda p: r.turn_in.at[p.h])
     up_attn_chain = chain("d_attn", r.d_attn, lambda place: r.blocks.at[2 * place + me.k])
     up_attn_relay = relay("d_attn", r.d_attn, lambda c: r.blocks.at[c])
-    mix_lane = lane("mix", lambda to: r.part_stage.at[to.h], lambda p: r.mix_in.at[p.h])
     dn_block = lambda c: rows_at(r.pool, c, R)
     dn_in = lambda j: rows_at(r.xin, j, R)
     sib_in = lambda j: rows_at(r.cot_v, j, R)
-    dn_lane = lane("dn", lambda to: dn_block(to.c), lambda p: dn_in(lax.div(p.c, 2)))
+    fold = lambda name, block, landing: Fold(z, me, CHAIN_GROUPS[name], r.total, block, landing, *sems("chain_", name))
+    part_fold = fold("part", lambda h: r.part_stage.at[h], lambda slot: r.part_in.at[slot])
+    mix_fold = fold("mix", lambda h: r.part_stage.at[h], lambda slot: r.mix_in.at[slot])
+    dn_fold = fold("dn", lambda place: dn_block(2 * place + me.k), dn_in)
     gc_lane = lane("gc", lambda to: r.gc_sum.at[to.c], lambda p: r.gc_in.at[p.c])
     gs_lane = lane("gs", lambda to: r.gs_sum.at[to.c], lambda p: r.gs_in.at[p.c])
     go_lane = lane("go", lambda to: rows_at(r.go_stage, to.f, rs), lambda p: r.go_in.at[p.f])
@@ -415,8 +482,7 @@
 
     wc_lane.wait_recv()
     small_lane.wait_recv()
-    wo_relay.start_own()
-    wo_chain.start()
+    wo_lane.start()
     tok_relay.start_own()
     tok_chain.start()
     cot_chain.start()
@@ -449,7 +515,6 @@
     times(C, lambda c: wc_column(c).wait_recv())
     times(C, lambda c: small_column(c).wait_recv())
     times(H, choose)
-    wo_chain.visit(lambda place, core: wo_column(2 * place + core).start(), wo_relay)
     gain_one = r.small_v[...].astype(jnp.float32).T[EXPERTS : EXPERTS + 1, :]
     gain_two = r.small_v[...].astype(jnp.float32).T[EXPERTS + 1 : EXPERTS + 2, :]
     head_of = lax.div(lane_of((R, LANES)), HEAD)
@@ -473,6 +538,10 @@
         r.v2[part, :] = jnp.where(head_of == 0, swapped, kv).astype(jnp.bfloat16)
     tok_chain.visit(project, tok_relay)
     gate_a_lane.start()
+    wo_lane.wait_recv()
+    times(J, lambda j: wo_column(2 * j + me.k).start())
+    dispatch_cot(me.h)
+    cot_chain.visit_some(dispatch_cot, 0, 2)
     tok_relay.wait_send()
 
     def attend(c):
@@ -496,9 +565,11 @@
     tok_chain.wait_send()
     att_lane.start()
     r.att_in[me.c] = r.att_stage[me.c]
-    cot_chain.visit(dispatch_cot)
+    cot_chain.visit_some(dispatch_cot, 2, min(4, 2 * (H - 1)))
+    times(J, lambda j: wo_column(2 * j + me.k).wait_recv())
+    times(J, wo_relay.start)
     att_lane.wait_recv()
-    times(C, lambda c: wo_column(c).wait_recv())
+    times(J, wo_relay.wait_recv)
     x = r.tok[...].astype(jnp.float32)
     mixed = jnp.zeros((R, D), jnp.float32)
     for c in range(C):
@@ -536,6 +607,7 @@
         at_slot(r.xin, h, me.p)[...] = r.stage[h, me.p]
         r.gin[h, me.p] = r.g_stage[h, me.p]
     rows_chain.visit(dispatch_rows)
+    cot_chain.visit_some(dispatch_cot, 4, 2 * (H - 1))
     gate_b_lane.start()
     up_lane.start()
     down_lane.start()
@@ -581,8 +653,7 @@
     grad_lanes[5].start()
     down_lane.wait_recv()
 
-    def chunk(j):
-        h = lax.rem(me.h + H - lax.rem(j + 1, H), H)
+    def chunk(h):
 
         def rows(t):
             some = pl.ds(pl.multiple_of(t * per, per), per)
@@ -612,7 +683,7 @@
         dg_plane(h).start()
         r.stage[h, me.p] = r.d_rows[h, me.p]
         r.dg_in[h, me.p] = r.dg_stage[h, me.p]
-    times(H, chunk)
+    part_fold.far_first(chunk)
 
     def cut(d):
         part = pl.ds(pl.multiple_of(d * 256, 256), 256)
@@ -627,44 +698,37 @@
     for copy in own_grads:
         copy.start()
 
-    def collect(j):
-        n = lax.rem(j + 1, H)
-        h = lax.rem(me.h + H - n, H)
+    def collect(h):
         back_plane(h).wait_recv()
         dg_plane(h).wait_recv()
-        part = tn(r.pick[h].reshape(P * CAP, R), r.stage[h].reshape(P * CAP, D))
+        r.total[...] = tn(r.pick[h].reshape(P * CAP, R), r.stage[h].reshape(P * CAP, D))
         r.turn_stage[h] = jnp.zeros((EXPERTS, R), jnp.float32)
 
         def gates_of(p):
             row = jnp.broadcast_to(r.dg_in[h, p, 0:1, 0:CAP], (8, CAP))
             r.turn_stage[h, pl.ds(z.expert(me, p), 1), :] = exact("nn", row, r.pick[h, p].astype(jnp.float32))[0:1, :]
         times(P, gates_of)
-        @pl.when(n > 0)
+        @pl.when(h != me.h)
         def _():
-            r.part_stage[h] = part.astype(jnp.bfloat16)
-            part_lane.start_one(H - n)
-            turn_lane.start_one(H - n)
-        @pl.when(n == 0)
-        def _():
-            r.d_mid[...] = part
-            r.turn_v[...] = jnp.zeros((LANES, R), jnp.float32)
-            r.turn_v[0:EXPERTS, :] = r.turn_stage[h]
-    times(H, collect)
+            part_fold.send(h)
+            turn_lane.start_one(lax.rem(h + H - me.h, H))
+    part_fold.far_first(collect)
+    r.turn_v[...] = jnp.zeros((LANES, R), jnp.float32)
+    r.turn_v[0:EXPERTS, :] = r.turn_stage[me.h]
     times(H, lambda h: out_plane(h).start())
     own_out = pltpu.make_async_copy(r.result.at[:, me.p], r.out_in.at[:, me.p], r.own_sem.at[7])
     own_out.start()
-    part_lane.wait_recv()
+    part_fold.finish()
     turn_lane.wait_recv()
 
     def add_part(n):
         h = lax.rem(me.h + n + 1, H)
-        r.d_mid[...] += r.part_in[h].astype(jnp.float32)
         r.turn_v[0:EXPERTS, :] += r.turn_in[h]
     times(H - 1, add_part)
     gts = r.gates_t[...].T
     dgs = r.turn_v[...].T
     d_log = gts * (dgs - jnp.sum(gts * dgs, axis=-1, keepdims=True))
-    d_h2 = r.d_mid[...] + exact("nt", d_log, r.small_v[...].astype(jnp.float32))
+    d_h2 = r.total[...] + exact("nt", d_log, r.small_v[...].astype(jnp.float32))
     mid = r.middle[...]
     inverse = lax.rsqrt(jnp.mean(mid * mid, axis=-1, keepdims=True) + norm_eps)
     n2 = mid * inverse
@@ -729,31 +793,28 @@
     def down_tokens(c):
         return nt(r.d_qkv[pl.ds(pl.multiple_of(c * R, R), R), :], r.wc_v[...])
 
-    def for_sibling(j):
-        c = 2 * j + 1 - me.k
+    def for_sibling(place):
+        c = 2 * place + 1 - me.k
         dn_block(c)[...] = down_tokens(c).astype(jnp.bfloat16)
-        sib_copy(j).start()
-    times(J, for_sibling)
-
-    def for_line(i):
-        n = lax.rem(i + 1, J)
-        to = z.peer("line", me, n)
-        dn = down_tokens(to.c)
-        j = lax.div(to.c, 2)
-        sib_copy(j).wait_recv()
-        dn_block(to.c)[...] = (dn + sib_in(j)[...].astype(jnp.float32)).astype(jnp.bfloat16)
-        @pl.when(n > 0)
+        sib_copy(place).start()
+    dn_fold.far_first(for_sibling)
+
+    def for_line(place):
+        dn = down_tokens(2 * place + me.k)
+        sib_copy(place).wait_recv()
+        r.total[...] = dn + sib_in(place)[...].astype(jnp.float32)
+        @pl.when(place != dn_fold.place)
         def _():
-            dn_lane.start_one(n)
-    times(J, for_line)
-    dn_in(lax.div(me.c, 2))[...] = dn_block(me.c)[...]
+            dn_fold.send(place)
+        @pl.when(place == dn_fold.place)
+        def _():
+            r.grad_tokens[...] = r.total[...]
+    dn_fold.far_first(for_line)
 
     own_out.wait()
-    part_lane.wait_send()
-
-    def mix(i):
-        n = lax.rem(i + 1, H)
-        h = lax.rem(me.h + H - n, H)
+    part_fold.wait_send()
+
+    def mix(h):
         out_plane(h).wait_recv()
         load = pltpu.make_async_copy(r.out_in.at[h], r.stage.at[h], r.own_sem.at[12])
         load.start()
@@ -767,14 +828,11 @@
         load.wait()
         rows = r.stage[h].reshape(P * CAP, D)
         total = tn(r.mix_hi[...].reshape(P * CAP, R), rows) + tn(r.mix_lo[...].reshape(P * CAP, R), rows)
-        r.part_stage[h] = total.astype(jnp.bfloat16)
-        @pl.when(n > 0)
+        r.total[...] = total
+        @pl.when(h != me.h)
         def _():
-            mix_lane.start_one(H - n)
-        @pl.when(n == 0)
-        def _():
-            r.grad_tokens[...] = total
-    times(H, mix)
+            mix_fold.send(h)
+    mix_fold.far_first(mix)
     grad_lanes[2].start()
     grad_lanes[3].start()
 
@@ -818,17 +876,12 @@
     ]
     for copy in own_sums:
         copy.start()
-    mix_lane.wait_recv()
-
-    def add_mix(n):
-        r.grad_tokens[...] += r.mix_in[lax.rem(me.h + n + 1, H)].astype(jnp.float32)
-    times(H - 1, add_mix)
-    r.output[...] = (r.middle[...] + residual_scale * r.grad_tokens[...]).astype(jnp.bfloat16)
-
-    dn_lane.wait_recv()
-    d_h1 = dn_in(0)[...].astype(jnp.float32)
-    for c in range(1, J):
-        d_h1 = d_h1 + dn_in(c)[...].astype(jnp.float32)
+    mix_fold.finish()
+    r.output[...] = (r.middle[...] + residual_scale * r.total[...]).astype(jnp.bfloat16)
+
+    r.total[...] = r.grad_tokens[...]
+    dn_fold.finish()
+    d_h1 = r.total[...]
     x = r.tok[...].astype(jnp.float32)
     inverse = lax.rsqrt(jnp.mean(x * x, axis=-1, keepdims=True) + norm_eps)
     n1 = x * inverse
@@ -839,16 +892,17 @@
     for last in grad_lanes:
         last.wait_recv()
     for last in [place_lane, wc_lane, small_lane, slot_lane, gate_a_lane, gate_b_lane, up_lane, down_lane, att_lane, gates_lane,
-                 turn_lane, mix_lane, dn_lane, gc_lane, gs_lane, go_lane] + grad_lanes:
+                 turn_lane, wo_lane, gc_lane, gs_lane, go_lane] + grad_lanes:
         last.wait_send()
-    for last in [wo_chain, cot_chain, rows_chain, up_attn_chain]:
+    for last in [cot_chain, rows_chain, up_attn_chain, mix_fold, dn_fold]:
         last.wait_send()
     for last in [wo_relay, up_attn_relay]:
         last.wait_send()
     times(J, lambda j: sib_copy(j).wait_send())
     for last in [g_plane, back_plane, dg_plane, out_plane]:
         times(H, lambda h, last=last: last(h).wait_send())
-    for last in [wc_column, small_column, wo_column, gc_column, gs_column]:
+    times(J, lambda j: wo_column(2 * j + me.k).wait_send())
+    for last in [wc_column, small_column, gc_column, gs_column]:
         times(C, lambda c, last=last: last(c).wait_send())
     for copy in own_grads + own_sums + [own_go]:
         copy.wait()
@@ -875,14 +929,14 @@
         cot_v=vmem((rows, D)), d_rows=vmem((H, P, CAP, D)), dg_stage=vmem((H, P, 8, LANES), f),
         dg_in=vmem((H, P, 8, LANES), f), hid=vmem((rows, ff)), d_gate=vmem((rows, ff)), d_up=vmem((rows, ff)),
         pool=vmem((max(rows, L), D)), g_col=vmem((tile, LANES), f), result=vmem((H, P, CAP, D)),
-        part_stage=vmem((H, R, D)), part_in=vmem((H, R, D)), turn_stage=vmem((H, EXPERTS, R), f),
+        part_stage=vmem((H, R, D)), part_in=vmem((H + 1, R, D)), turn_stage=vmem((H, EXPERTS, R), f),
         turn_in=vmem((H, EXPERTS, R), f), turn_v=vmem((LANES, R), f), d_mid=vmem((R, D), f), d_attn=vmem((R, D)),
         g_small=vmem((D, LANES), f), g_down=vmem((D, ff)), gain_v=vmem((LANES, D), f), ds_v=vmem((heads, L)), p_v=vmem((heads, L)),
         q_v=vmem((heads, LANES)), dm_v=vmem((heads, LANES)), dk_acc=vmem((L, LANES), f), dv_acc=vmem((L, LANES), f),
         d_qkv=vmem((L, 2 * LANES)),
         gc_stage=vmem((D, 2 * LANES)), go_stage=vmem((LANES, D)), gs_stage=vmem((D, LANES)), gc_x=vmem((F, C, rs, 2 * LANES)),
         gs_x=vmem((F, C, rs, LANES)), gc_sum=vmem((C, rs, 2 * LANES)), gs_sum=vmem((C, rs, LANES)), mix_hi=vmem((P, CAP, R)),
-        mix_lo=vmem((P, CAP, R)), mix_in=vmem((H, R, D)), own_sem=pltpu.SemaphoreType.DMA((16,)),
+        mix_lo=vmem((P, CAP, R)), mix_in=vmem((H + 1, R, D)), total=vmem((R, D), f), own_sem=pltpu.SemaphoreType.DMA((16,)),
         own_cols=pltpu.SemaphoreType.DMA((2, C)))
     both = ("_send", "_recv")
     scratch |= {"lane_" + n + b: pltpu.SemaphoreType.DMA((z.count(g),)) for n, g in LANE_GROUPS.items() for b in both}

time: 356 us -> 341 us (0.958); the launches traced: 353 us -> 334 us
  Pallas kernels: 327 us -> 308 us
    pallas_call x1, Pallas kernels: 327 us -> 308 us  [layer_call(): pl.pallas_call(functools.partial(layer_kernel, z, R, dc, tile, names), na...]
where the time goes in v2:
time: 341 us; the launch traced here: 334 us
  Pallas kernels  308 us (90%)
  local copies, waits for them, and re-layouts  15.5 us (5%)
  other arithmetic  10.3 us (3%)
    pallas_call x1, Pallas kernels, layer_call(): pl.pallas_call(functools.partial(layer_kernel, z, R, dc, tile, names), na...  308 us
    unnamed x11, local copies, waits for them, and re-layouts  7 us

profile of v2, /device:TPU:9, one launch (start us, length us, event | category | flops | bytes accessed | tf_op | source)
XLA Modules:
  0.0 334.3 jit_solution(7246632337142704379)
XLA Ops:
  0.7 0.1 pad.3.clone
  0.7 1.2 broadcast_in_dim.23.refs_1_
  2.0 0.7 copy.36
  2.7 0.8 copy.37
  3.5 1.4 maximum_maximum_fusion.refs_6_
  4.9 0.9 copy_bitcast_fusion.1
  5.7 0.9 reshape_broadcast_in_dim_reshape.6
  6.6 0.9 reshape_broadcast_in_dim_reshape.7
  7.5 0.7 maximum_bitcast_fusion.refs_5_
  8.2 1.4 copy.32
  9.7 2.3 copy.38
  11.9 307.7 %layer.1 = (bf16[128,1024]{1,0:T(8,128)(2,1)}, f32[128,1024]{1,0:T(8,128)}, bf16[8,32,256]{2,1,0:T(8,128)(2,1)}, bf16[8,32,128]{2,1,0:T(8,128)(2,1)}, bf16[4,32,...) custom-call(bf16[128,1024]{1,0:T(8,128)(2,1)} %bitcast.42, ...), custom_call_target="tpu_custom_call" | custom-call | tf_op jit(solution)/shard_map/layer/pallas_call | solution.py:950
  319.6 0.9 convert_reduce_fusion.1
  320.5 0.0 copy-start.2
  320.5 0.7 slice_reduce_fusion
  321.2 1.7 convert_reduce_fusion
  322.9 0.9 convert_element_type.35
  323.8 0.7 copy_bitcast_fusion
  324.5 0.1 slice_bitcast_fusion
  324.6 0.1 copy.41
  324.6 0.7 reshape.66
  325.4 0.1 copy.40
  325.4 0.7 reshape.65
  326.2 4.8 %convert_bitcast_fusion = (f32[8,512,128]{1,2,0:T(8,128)S(1)}, f32[8,128,512]{2,1,0:T(8,128)}, f32[8,128,512]{2,1,0:T(8,128)}) fusion(bf16[3,1,8,128,512]{4,3,2,1,0:T(8,128)(2,1)} %get-tuple-element.23), kind=kLoop, calls=%fused_computation | loop fusion | flops 1572864 | bytes 9437184 | tf_op jit(solution)/shard_map/transpose | solution.py:992
  330.9 0.0 copy-done.2
  330.9 0.0 copy-start.1
  330.9 0.0 copy-start
  330.9 1.8 copy.42
  332.8 0.0 copy-done.1
  332.8 0.7 copy.49
  333.5 0.0 copy-done
  333.5 0.8 copy.50
  (3 shorter events, 0.0 us)
Async XLA Ops:
  320.5 10.4 %copy-start.2 = (f32[32,128]{1,0:T(8,128)}, f32[32,128]{1,0:T(8,128)S(1)}, u32[]{:S(2)}) copy-start(f32[32,128]{1,0:T(8,128)S(1)} %convert_reduce_fusion.1) | copy-start | bytes 49156
  330.9 1.8 copy-start.1
  330.9 2.5 copy-start

commit v3 on v2

--- a/solution.py
+++ b/solution.py
@@ -396,7 +396,7 @@
 
     tok_chain = chain("tok", r.tok, lambda place: r.blocks.at[2 * place + me.k])
     tok_relay = relay("tok", r.tok, lambda c: r.blocks.at[c])
-    place_lane = lane("place", lambda to: r.place, lambda p: r.place_all.at[p.c])
+    place_lane = lane("place", lambda to: r.place_all.at[me.c], lambda p: r.place_all.at[p.c])
     wc_lane = lane("wc", lambda to: r.w_pack.at[to.c], lambda p: rows_at(r.wc_v, p.w, rs))
     small_lane = lane("small", lambda to: r.small, lambda p: rows_at(r.small_v, p.w, rs))
     wo_lane = lane("wo", lambda to: r.w_out, lambda p: rows_at(r.wo_v, p.w, rs))
@@ -450,6 +450,7 @@
             device_id=(me.c + 1 - 2 * me.k, me.f), device_id_type=MESH)
 
     meet(z, me, ["ctx", "plane", "fsdp"])
+    r.place_all[me.c] = jnp.broadcast_to(r.place[...], (8, R))
     wc_lane.start()
     small_lane.start()
     place_lane.start()
@@ -466,16 +467,15 @@
     for copy in own + own_weights:
         copy.start()
     r.blocks[me.c] = r.tok[...]
-    r.place_all[me.c] = r.place[...]
     r.cot_all[me.h] = r.cot[...]
 
-    named = jnp.zeros((R, LANES), jnp.float32)
+    row_id = lax.broadcasted_iota(jnp.int32, (LANES, R), 0)
+    named = jnp.zeros((LANES, R), jnp.float32)
     for j in range(TOP):
-        named = jnp.where(r.routes[:, j : j + 1] == lane_of((R, LANES)), 1.0, named)
-    row_id = lax.broadcasted_iota(jnp.int32, (R, R), 0)
-    before = jnp.where(row_id > lane_of((R, R)), 1.0, 0.0).astype(jnp.bfloat16)
-    slot = nn(before, named.astype(jnp.bfloat16))
-    r.slot_t[...] = jnp.where(named > 0.5, slot, -1.0).T
+        named = jnp.where(r.routes[j : j + 1, :] == row_id, 1.0, named)
+    before = jnp.where(row_id < lane_of((R, R)), 1.0, 0.0).astype(jnp.bfloat16)
+    slot = nn(named.astype(jnp.bfloat16), before)
+    r.slot_t[...] = jnp.where(named > 0.5, slot, -1.0)
     r.slot_all[me.h] = r.slot_t[0:EXPERTS, :]
     slot_lane.start()
     slot_id = lax.broadcasted_iota(jnp.int32, (CAP, R), 0).astype(jnp.float32)
@@ -536,11 +536,11 @@
         swapped = pltpu.roll(kv, HEAD, 1)
         r.k2[part, :] = jnp.where(head_of == 0, kv, swapped).astype(jnp.bfloat16)
         r.v2[part, :] = jnp.where(head_of == 0, swapped, kv).astype(jnp.bfloat16)
+    dispatch_cot(me.h)
+    wo_lane.wait_recv()
+    times(J, lambda j: wo_column(2 * j + me.k).start())
     tok_chain.visit(project, tok_relay)
     gate_a_lane.start()
-    wo_lane.wait_recv()
-    times(J, lambda j: wo_column(2 * j + me.k).start())
-    dispatch_cot(me.h)
     cot_chain.visit_some(dispatch_cot, 0, 2)
     tok_relay.wait_send()
 
@@ -698,6 +698,13 @@
     for copy in own_grads:
         copy.start()
 
+    def trickle(q):
+        for i, bulk in enumerate(grad_lanes[1:4]):
+            n = q - i * (C - 1) + 1
+            @pl.when(jnp.logical_and(n > 0, n < C))
+            def _(bulk=bulk, n=n):
+                bulk.start_one(n)
+
     def collect(h):
         back_plane(h).wait_recv()
         dg_plane(h).wait_recv()
@@ -749,6 +756,7 @@
 
     def attend_back(place, core):
         c = 2 * place + core
+        trickle(2 * H + c)
         part = pl.ds(pl.multiple_of(c * R, R), R)
         q = r.q_all[part, :]
         d_mix = nt(r.blocks[c], wo_c[...])
@@ -778,7 +786,6 @@
         cosine, sine = rope_tables(places, r.freq[0:1, :])
         r.d_qkv[part, 0:LANES] = rope(dq, cosine, -sine).astype(jnp.bfloat16)
     up_attn_chain.visit(attend_back, up_attn_relay)
-    grad_lanes[1].start()
 
     def finish_kv(c):
         part = pl.ds(pl.multiple_of(c * R, R), R)
@@ -833,8 +840,8 @@
         def _():
             mix_fold.send(h)
     mix_fold.far_first(mix)
-    grad_lanes[2].start()
-    grad_lanes[3].start()
+    times(3 * (C - 1), trickle, 2 * H + C)
+    times(2 * H, trickle)
 
     def weights(d):
         part = pl.ds(pl.multiple_of(d * 256, 256), 256)
@@ -876,6 +883,17 @@
     ]
     for copy in own_sums:
         copy.start()
+    for last in [place_lane, wc_lane, small_lane, slot_lane, gate_a_lane, gate_b_lane, up_lane, down_lane, att_lane, gates_lane,
+                 turn_lane, wo_lane, *grad_lanes[4:]]:
+        last.wait_send()
+    for last in [cot_chain, rows_chain, up_attn_chain, wo_relay, up_attn_relay]:
+        last.wait_send()
+    times(J, lambda j: sib_copy(j).wait_send())
+    for last in [g_plane, back_plane, dg_plane, out_plane]:
+        times(H, lambda h, last=last: last(h).wait_send())
+    times(J, lambda j: wo_column(2 * j + me.k).wait_send())
+    for last in [wc_column, small_column, gc_column, gs_column]:
+        times(C, lambda c, last=last: last(c).wait_send())
     mix_fold.finish()
     r.output[...] = (r.middle[...] + residual_scale * r.total[...]).astype(jnp.bfloat16)
 
@@ -891,19 +909,10 @@
         last.wait_recv()
     for last in grad_lanes:
         last.wait_recv()
-    for last in [place_lane, wc_lane, small_lane, slot_lane, gate_a_lane, gate_b_lane, up_lane, down_lane, att_lane, gates_lane,
-                 turn_lane, wo_lane, gc_lane, gs_lane, go_lane] + grad_lanes:
+    for last in [gc_lane, gs_lane, go_lane] + grad_lanes[:4]:
         last.wait_send()
-    for last in [cot_chain, rows_chain, up_attn_chain, mix_fold, dn_fold]:
+    for last in [mix_fold, dn_fold]:
         last.wait_send()
-    for last in [wo_relay, up_attn_relay]:
-        last.wait_send()
-    times(J, lambda j: sib_copy(j).wait_send())
-    for last in [g_plane, back_plane, dg_plane, out_plane]:
-        times(H, lambda h, last=last: last(h).wait_send())
-    times(J, lambda j: wo_column(2 * j + me.k).wait_send())
-    for last in [wc_column, small_column, gc_column, gs_column]:
-        times(C, lambda c, last=last: last(c).wait_send())
     for copy in own_grads + own_sums + [own_go]:
         copy.wait()
 
@@ -970,10 +979,9 @@
     w_pack = jnp.concatenate([heads_q, heads_k, heads_v], axis=2).transpose(1, 0, 2)
     small = jnp.concatenate(
         [w_router, norm_first[:, None], norm_second[:, None], jnp.zeros((rs, 128 - EXPERTS - 2), jnp.bfloat16)], axis=1)
-    place_pack = jnp.broadcast_to(positions[0][None, :], (8, R))
     w_downt = w_down.transpose(0, 2, 1)
     output, grad_tokens, gc_in, gs_in, go_in, gw_in = layer_call(
-        z, R, ff, dc, tokens[0], place_pack, routes[0], cotangent[0], w_pack, small, w_out, w_gate, w_up, w_downt)
+        z, R, ff, dc, tokens[0], positions, routes[0].T, cotangent[0], w_pack, small, w_out, w_gate, w_up, w_downt)
     gc = f32(gc_in)
     join = lambda a: a.reshape(KV_HEADS, z.share, rs, HEAD).sum(axis=1).transpose(1, 0, 2).reshape(rs, KV_HEADS * HEAD)
     gs = jnp.sum(f32(gs_in), axis=0)

time: 341 us -> 331 us (0.971); the launches traced: 334 us -> 328 us
  Pallas kernels: 308 us -> 304 us
    unnamed x11 -> x10, local copies, waits for them, and re-layouts: 7 us -> 5.58 us
where the time goes in v3:
time: 331 us; the launch traced here: 328 us
  Pallas kernels  304 us (92%)
  local copies, waits for them, and re-layouts  12.8 us (4%)
  other arithmetic  10.3 us (3%)
    pallas_call x1, Pallas kernels, layer_call(): pl.pallas_call(functools.partial(layer_kernel, z, R, dc, tile, names), na...  304 us

profile of v3, /device:TPU:9, one launch (start us, length us, event | category | flops | bytes accessed | tf_op | source)
XLA Modules:
  0.0 328.2 jit_solution(4405340519141877110)
XLA Ops:
  0.7 0.1 pad.3.clone
  0.7 0.7 copy.34
  1.5 0.8 copy.35
  2.2 1.4 maximum_maximum_fusion.refs_6_
  3.6 0.9 copy_bitcast_fusion.1
  4.5 0.9 reshape_broadcast_in_dim_reshape.6
  5.4 0.9 reshape_broadcast_in_dim_reshape.7
  6.2 0.7 maximum_bitcast_fusion.refs_5_
  7.0 2.3 copy.36
  9.3 304.3 %layer.1 = (bf16[128,1024]{1,0:T(8,128)(2,1)}, f32[128,1024]{1,0:T(8,128)}, bf16[8,32,256]{2,1,0:T(8,128)(2,1)}, bf16[8,32,128]{2,1,0:T(8,128)(2,1)}, bf16[4,32,...) custom-call(bf16[128,1024]{1,0:T(8,128)(2,1)} %bitcast.41, ...), custom_call_target="tpu_custom_call" | custom-call | tf_op jit(solution)/shard_map/layer/pallas_call | solution.py:959
  313.6 0.9 convert_reduce_fusion.1
  314.5 0.0 copy-start.2
  314.5 0.7 slice_reduce_fusion
  315.2 1.7 convert_reduce_fusion
  316.8 0.9 convert_element_type.35
  317.7 0.7 copy_bitcast_fusion
  318.4 0.1 slice_bitcast_fusion
  318.5 0.1 copy.39
  318.6 0.7 reshape.66
  319.3 0.1 copy.38
  319.4 0.7 reshape.65
  320.1 4.7 %convert_bitcast_fusion = (f32[8,512,128]{1,2,0:T(8,128)S(1)}, f32[8,128,512]{2,1,0:T(8,128)}, f32[8,128,512]{2,1,0:T(8,128)}) fusion(bf16[3,1,8,128,512]{4,3,2,1,0:T(8,128)(2,1)} %get-tuple-element.23), kind=kLoop, calls=%fused_computation | loop fusion | flops 1572864 | bytes 9437184 | tf_op jit(solution)/shard_map/transpose | solution.py:1000
  324.8 0.0 copy-done.2
  324.9 0.0 copy-start.1
  324.9 0.0 copy-start
  324.9 1.8 copy.40
  326.7 0.0 copy-done.1
  326.7 0.7 copy.47
  327.4 0.0 copy-done
  327.4 0.8 copy.48
  (3 shorter events, 0.0 us)
Async XLA Ops:
  314.5 10.4 %copy-start.2 = (f32[32,128]{1,0:T(8,128)}, f32[32,128]{1,0:T(8,128)S(1)}, u32[]{:S(2)}) copy-start(f32[32,128]{1,0:T(8,128)S(1)} %convert_reduce_fusion.1) | copy-start | bytes 49156
  324.9 1.8 copy-start.1
  324.9 2.5 copy-start

commit v4 on v3

--- a/solution.py
+++ b/solution.py
@@ -429,12 +429,15 @@
     gather = lambda name, stage, landing: column(
         name, lambda c, to: rows_at(stage, c * F + to.f, rs), lambda c, p: landing.at[p.f, c])
     gc_column, gs_column = gather("gc", r.gc_stage, r.gc_x), gather("gs", r.gs_stage, r.gs_x)
-    grad_of = lambda j, c: rows_at(r.g_down, c, dc) if j == 2 else r.wv.at[j, c]
+    halves = (pl.ds(0, r.g_down.shape[1] // 2), pl.ds(r.g_down.shape[1] // 2, r.g_down.shape[1] // 2))
     grad_lanes = [
         lane("grad" + str(2 * j + i),
-             lambda to, j=j, i=i: grad_of(j, to.c).at[(low, high)[i]],
+             lambda to, j=j, i=i: r.wv.at[j, to.c, (low, high)[i]],
              lambda p, j=j, i=i: r.gw_in.at[j, p.s, p.m, (low, high)[i]])
-        for j in range(3) for i in range(2)
+        for j in range(2) for i in range(2)
+    ] + [
+        lane("grad" + str(4 + i), lambda to, i=i: r.g_down.at[to.c, halves[i]], lambda p, i=i: r.gd_in.at[p.s, p.m, halves[i]])
+        for i in range(2)
     ]
     cot_plane = plane("cot", r.d_rows, r.cot_v)
     row_plane = plane("row", r.stage, r.xin)
@@ -647,7 +650,9 @@
 
     def cut_down(d):
         part = pl.ds(pl.multiple_of(d * 256, 256), 256)
-        r.g_down[part, :] = tn(r.pool[pl.ds(0, H * P * CAP), part], r.hid[...]).astype(jnp.bfloat16)
+        total = tn(r.hid[...], r.pool[pl.ds(0, H * P * CAP), part]).astype(jnp.bfloat16)
+        for i in range(256 // dc):
+            r.g_down[d * (256 // dc) + i] = total[:, i * dc : (i + 1) * dc]
     times(D // 256, cut_down)
     grad_lanes[4].start()
     grad_lanes[5].start()
@@ -693,7 +698,9 @@
     times(D // 256, cut)
     grad_lanes[0].start()
     own_grads = [
-        pltpu.make_async_copy(grad_of(j, me.c), r.gw_in.at[j, me.s, me.m], r.own_sem.at[8 + j]) for j in range(3)
+        pltpu.make_async_copy(source, landing, r.own_sem.at[8 + j]) for j, (source, landing) in enumerate([
+            (r.wv.at[0, me.c], r.gw_in.at[0, me.s, me.m]), (r.wv.at[1, me.c], r.gw_in.at[1, me.s, me.m]),
+            (r.g_down.at[me.c], r.gd_in.at[me.s, me.m])])
     ]
     for copy in own_grads:
         copy.start()
@@ -925,7 +932,8 @@
                small=(small, 0), w_out=(w_out, 0), w_gate=(w_gate, 0), w_up=(w_up, 0), w_downt=(w_downt, 0))
     outs = dict(
         output=(shape_of((R, D)), 1), grad_tokens=(shape_of((R, D), f), 1), gc_in=(shape_of((C, rs, 2 * LANES)), 0),
-        gs_in=(shape_of((C, rs, LANES)), 0), go_in=(shape_of((F, rs, D)), 0), gw_in=(shape_of((3, S, z.G, dc, ff)), 0),
+        gs_in=(shape_of((C, rs, LANES)), 0), go_in=(shape_of((F, rs, D)), 0), gw_in=(shape_of((2, S, z.G, dc, ff)), 0),
+        gd_in=(shape_of((S, z.G, ff, dc)), 0),
         out_in=(shape_of((H, P, CAP, D)), 0))
     scratch = dict(
         blocks=vmem((C, R, D)), place_all=vmem((C, 8, R), jnp.int32), wc_v=vmem((D, 2 * LANES)), small_v=vmem((D, LANES)),
@@ -940,7 +948,7 @@
         pool=vmem((max(rows, L), D)), g_col=vmem((tile, LANES), f), result=vmem((H, P, CAP, D)),
         part_stage=vmem((H, R, D)), part_in=vmem((H + 1, R, D)), turn_stage=vmem((H, EXPERTS, R), f),
         turn_in=vmem((H, EXPERTS, R), f), turn_v=vmem((LANES, R), f), d_mid=vmem((R, D), f), d_attn=vmem((R, D)),
-        g_small=vmem((D, LANES), f), g_down=vmem((D, ff)), gain_v=vmem((LANES, D), f), ds_v=vmem((heads, L)), p_v=vmem((heads, L)),
+        g_small=vmem((D, LANES), f), g_down=vmem((C, ff, dc)), gain_v=vmem((LANES, D), f), ds_v=vmem((heads, L)), p_v=vmem((heads, L)),
         q_v=vmem((heads, LANES)), dm_v=vmem((heads, LANES)), dk_acc=vmem((L, LANES), f), dv_acc=vmem((L, LANES), f),
         d_qkv=vmem((L, 2 * LANES)),
         gc_stage=vmem((D, 2 * LANES)), go_stage=vmem((LANES, D)), gs_stage=vmem((D, LANES)), gc_x=vmem((F, C, rs, 2 * LANES)),
@@ -962,7 +970,7 @@
         out_specs=[space(fast) for _, fast in outs.values()], scratch_shapes=list(scratch.values()),
         compiler_params=pltpu.CompilerParams(collective_id=0, has_side_effects=True, vmem_limit_bytes=67043328),
     )(*[a for a, _ in ins.values()])
-    return results[:6]
+    return results[:7]
 
 
 def local(z, tokens, norm_first, w_query, w_key, w_value, w_out, norm_second, w_router,
@@ -980,7 +988,7 @@
     small = jnp.concatenate(
         [w_router, norm_first[:, None], norm_second[:, None], jnp.zeros((rs, 128 - EXPERTS - 2), jnp.bfloat16)], axis=1)
     w_downt = w_down.transpose(0, 2, 1)
-    output, grad_tokens, gc_in, gs_in, go_in, gw_in = layer_call(
+    output, grad_tokens, gc_in, gs_in, go_in, gw_in, gd_in = layer_call(
         z, R, ff, dc, tokens[0], positions, routes[0].T, cotangent[0], w_pack, small, w_out, w_gate, w_up, w_downt)
     gc = f32(gc_in)
     join = lambda a: a.reshape(KV_HEADS, z.share, rs, HEAD).sum(axis=1).transpose(1, 0, 2).reshape(rs, KV_HEADS * HEAD)
@@ -997,7 +1005,7 @@
         gs[:, :EXPERTS],
         jnp.sum(f32(gw_in[0]), axis=0),
         jnp.sum(f32(gw_in[1]), axis=0),
-        jnp.sum(f32(gw_in[2]), axis=0).transpose(0, 2, 1),
+        jnp.sum(f32(gd_in), axis=0),
     )
 
 

time: 331 us -> 329 us (level)
    transpose x1 -> x0, other arithmetic: 4.72 us -> none  [local(): jnp.sum(f32(gw_in[2]), axis=0).transpose(0, 2, 1)]
where the time goes in v4:
time: 329 us; the launch traced here: 326 us
  Pallas kernels  304 us (92%)
  local copies, waits for them, and re-layouts  11 us (3%)
  other arithmetic  9.74 us (3%)
    pallas_call x1, Pallas kernels, layer_call(): pl.pallas_call(functools.partial(layer_kernel, z, R, dc, tile, names), na...  304 us

profile of v4, /device:TPU:9, one launch (start us, length us, event | category | flops | bytes accessed | tf_op | source)
XLA Modules:
  0.0 325.7 jit_solution(17521192116476246376)
XLA Ops:
  0.6 0.9 reshape_broadcast_in_dim_reshape.7
  1.5 0.9 reshape_broadcast_in_dim_reshape.6
  2.4 0.9 copy_bitcast_fusion.1
  3.3 0.7 maximum_bitcast_fusion.refs_5_
  4.0 0.7 copy.34
  4.8 0.8 copy.33
  5.5 0.1 pad.3.clone
  5.6 1.4 maximum_maximum_fusion.refs_6_
  7.0 2.3 copy.35
  9.2 304.2 %layer.1 = (bf16[128,1024]{1,0:T(8,128)(2,1)}, f32[128,1024]{1,0:T(8,128)}, bf16[8,32,256]{2,1,0:T(8,128)(2,1)}, bf16[8,32,128]{2,1,0:T(8,128)(2,1)}, bf16[4,32,...) custom-call(bf16[128,1024]{1,0:T(8,128)(2,1)} %bitcast.39, ...), custom_call_target="tpu_custom_call" | custom-call | tf_op jit(solution)/shard_map/layer/pallas_call | solution.py:967
  313.4 0.0 copy-start
  313.4 1.0 convert_reduce_fusion.1
  314.4 0.0 copy-start.4
  314.5 0.7 slice_reduce_fusion
  315.2 0.9 convert_element_type.29
  316.1 0.7 copy_bitcast_fusion
  316.8 0.1 slice_bitcast_fusion
  316.8 0.1 copy.37
  316.9 0.7 reshape.60
  317.7 0.1 copy.38
  317.7 0.7 reshape.61
  318.5 1.7 convert_reduce_fusion
  320.1 0.0 copy-done
  320.1 0.0 copy-start.1
  320.1 2.6 bitcast_convert_fusion.1
  322.7 0.0 copy-done.4
  322.7 0.0 copy-start.3
  322.7 0.0 copy-start.2
  322.7 0.0 copy-done.1
  322.7 1.5 bitcast_convert_fusion
  324.2 0.0 copy-done.3
  324.2 0.7 copy.45
  324.9 0.0 copy-done.2
  324.9 0.8 copy.46
  (3 shorter events, 0.0 us)
Async XLA Ops:
  313.4 6.7 %copy-start = (bf16[2,1,8,128,512]{4,3,2,1,0:T(8,128)(2,1)S(1)}, bf16[2,1,8,128,512]{4,3,2,1,0:T(8,128)(2,1)}, u32[]{:S(2)}) copy-start(bf16[2,1,8,128,512]{4,3,2,1,0:T(8,128)(2,1)} %get-tuple-element.24) | copy-start | bytes 6291460
  314.4 8.3 %copy-start.4 = (f32[32,128]{1,0:T(8,128)}, f32[32,128]{1,0:T(8,128)S(1)}, u32[]{:S(2)}) copy-start(f32[32,128]{1,0:T(8,128)S(1)} %convert_reduce_fusion.1) | copy-start | bytes 49156
  320.1 2.6 copy-start.1
  322.7 1.5 copy-start.3
  322.7 2.2 copy-start.2
